TPU v7x, 32 devices: a 4x4x1 block of a 4x4x8 slice. The times are simulated.
32 devices in a mesh: dp: 1 (over z), ei: 4 (over y), eo: 8 (over x, core).
Axes of the slice: x: 4, y: 4, z: 1, core: 2. Of those that a mesh axis runs over, the one named last changes fastest.
The devices are a block of a 4x4x8 slice.
Arguments:
- x_in: bfloat16 [8192, 1024], P(('dp', 'ei', 'eo'))
- expert_idx: int32 [8192, 8], P(('dp', 'ei', 'eo'))
- gate_val: float32 [8192, 8], P(('dp', 'ei', 'eo'))
- w_gate: bfloat16 [32, 1024, 512], P(('ei', 'eo'))
- w_up: bfloat16 [32, 1024, 512], P(('ei', 'eo'))
- w_down: bfloat16 [32, 512, 1024], P(('ei', 'eo'))
- dy_in: bfloat16 [8192, 1024], P(('dp', 'ei', 'eo'))
Outputs:
- output 1: bfloat16 [8192, 1024], P(('dp', 'ei', 'eo'))
- output 2: bfloat16 [8192, 1024], P(('dp', 'ei', 'eo'))
- output 3: float32 [8192, 8], P(('dp', 'ei', 'eo'))
- output 4: float32 [32, 1024, 512], P(('dp', 'ei', 'eo'))
- output 5: float32 [32, 1024, 512], P(('dp', 'ei', 'eo'))
- output 6: float32 [32, 512, 1024], P(('dp', 'ei', 'eo'))
All inputs are finite; a program needn't handle non-finite values.
Results may differ from a plain program's by a relative error of at most 0.00784527.
Values are sent between devices in bfloat16 or wider.
A program may use at most 768 MiB of HBM per device.

v0:
```python
import jax
import jax.numpy as jnp
from jax import lax
from jax.sharding import PartitionSpec as P

SKEW_FACTOR = 4


def route_slots(dev_idx, experts, group_devs, capacity):
    tok_count, top_k = dev_idx.shape
    n_assign = tok_count * top_k
    flat_exp = dev_idx.reshape(n_assign)
    sort_order = jnp.argsort(flat_exp, stable=True).astype(jnp.int32)
    sorted_exp = flat_exp[sort_order]
    counts = jax.ops.segment_sum(jnp.ones((n_assign,), jnp.int32), flat_exp, num_segments=experts)
    starts = jnp.cumsum(counts) - counts
    within = jnp.arange(n_assign, dtype=jnp.int32) - starts[sorted_exp]
    exp_local = experts // group_devs
    slot_sorted = (((sorted_exp % exp_local) * group_devs + sorted_exp // exp_local) * capacity + within).astype(jnp.int32)
    slot_of = jnp.zeros((n_assign,), jnp.int32).at[sort_order].set(slot_sorted)
    slot_owner = jnp.full((experts * capacity,), -1, jnp.int32).at[slot_sorted].set(sort_order)
    return slot_of, slot_owner


def expert_forward(x_rows, wg_loc, wu_loc, wd_loc):
    pre_gate = jnp.einsum('ecd,edf->ecf', x_rows, wg_loc, preferred_element_type=jnp.float32)
    pre_up = jnp.einsum('ecd,edf->ecf', x_rows, wu_loc, preferred_element_type=jnp.float32)
    sig_gate = jax.nn.sigmoid(pre_gate)
    hidden = (pre_gate * sig_gate * pre_up).astype(jnp.bfloat16)
    out_rows = jnp.einsum('ecf,efd->ecd', hidden, wd_loc, preferred_element_type=jnp.float32).astype(jnp.bfloat16)
    return out_rows, (pre_gate, pre_up, sig_gate, hidden)


def expert_backward(x_rows, do_rows, saved_acts, wg_loc, wu_loc, wd_loc):
    pre_gate, pre_up, sig_gate, hidden = saved_acts
    silu_gate = pre_gate * sig_gate
    dw_down = jnp.einsum('ecf,ecd->efd', hidden, do_rows, preferred_element_type=jnp.float32)
    d_hidden = jnp.einsum('ecd,efd->ecf', do_rows, wd_loc, preferred_element_type=jnp.float32)
    d_gate = (d_hidden * pre_up * sig_gate * (1.0 + pre_gate * (1.0 - sig_gate))).astype(jnp.bfloat16)
    d_up = (d_hidden * silu_gate).astype(jnp.bfloat16)
    dw_gate = jnp.einsum('ecd,ecf->edf', x_rows, d_gate, preferred_element_type=jnp.float32)
    dw_up = jnp.einsum('ecd,ecf->edf', x_rows, d_up, preferred_element_type=jnp.float32)
    dx_rows = (jnp.einsum('ecf,edf->ecd', d_gate, wg_loc, preferred_element_type=jnp.float32) + jnp.einsum('ecf,edf->ecd', d_up, wu_loc, preferred_element_type=jnp.float32)).astype(jnp.bfloat16)
    return dx_rows, dw_gate, dw_up, dw_down


def to_experts(row_data, exp_local, ei_size, eo_size, capacity):
    row_width = row_data.shape[-1]
    buffer = row_data.reshape(exp_local, ei_size, eo_size, capacity, row_width)
    buffer = lax.all_to_all(buffer, 'eo', 2, 2, tiled=True)
    buffer = lax.all_to_all(buffer, 'ei', 1, 1, tiled=True)
    return buffer.reshape(exp_local, ei_size * eo_size * capacity, row_width)


def to_tokens(row_data, ei_size, eo_size, capacity):
    exp_local, n_rows, row_width = row_data.shape
    buffer = row_data.reshape(exp_local, ei_size, eo_size, capacity, row_width)
    buffer = lax.all_to_all(buffer, 'ei', 1, 1, tiled=True)
    buffer = lax.all_to_all(buffer, 'eo', 2, 2, tiled=True)
    return buffer.reshape(exp_local * n_rows, row_width)


def solution(mesh):
    ei_size = mesh.shape['ei']
    eo_size = mesh.shape['eo']
    group_devs = ei_size * eo_size
    tok_spec = P(('dp', 'ei', 'eo'), None)
    weight_spec = P(('ei', 'eo'), None, None)
    grad_spec = P(('dp', 'ei', 'eo'), None, None)

    def device_layer(x_loc, idx_loc, gate_loc, wg_loc, wu_loc, wd_loc, dy_loc):
        tok_count, top_k = idx_loc.shape
        d_model = x_loc.shape[1]
        exp_local = wg_loc.shape[0]
        experts = exp_local * group_devs
        capacity = SKEW_FACTOR * ((tok_count * top_k + experts - 1) // experts)
        slot_of, slot_owner = route_slots(idx_loc, experts, group_devs, capacity)
        has_row = slot_owner >= 0
        safe_owner = jnp.where(has_row, slot_owner, 0)
        tok_of_slot = safe_owner // top_k
        x_recv = to_experts(x_loc[tok_of_slot], exp_local, ei_size, eo_size, capacity)
        out_rows, saved_acts = expert_forward(x_recv, wg_loc, wu_loc, wd_loc)
        out_back = to_tokens(out_rows, ei_size, eo_size, capacity)
        out_tok = out_back[slot_of].reshape(tok_count, top_k, d_model)
        y_loc = jnp.sum(gate_loc[:, :, None] * out_tok, axis=1).astype(jnp.bfloat16)
        dgate_loc = jnp.einsum('td,tkd->tk', dy_loc, out_tok, preferred_element_type=jnp.float32)
        slot_gate = jnp.where(has_row, gate_loc.reshape(tok_count * top_k)[safe_owner], 0.0)
        do_send = (slot_gate[:, None] * dy_loc[tok_of_slot]).astype(jnp.bfloat16)
        do_recv = to_experts(do_send, exp_local, ei_size, eo_size, capacity)
        dx_rows, dw_gate, dw_up, dw_down = expert_backward(x_recv, do_recv, saved_acts, wg_loc, wu_loc, wd_loc)
        dx_back = to_tokens(dx_rows, ei_size, eo_size, capacity)
        dx_loc = jnp.sum(dx_back[slot_of].reshape(tok_count, top_k, d_model).astype(jnp.float32), axis=1).astype(jnp.bfloat16)
        return y_loc, dx_loc, dgate_loc, dw_gate, dw_up, dw_down

    return jax.shard_map(device_layer, mesh=mesh, in_specs=(tok_spec, tok_spec, tok_spec, weight_spec, weight_spec, weight_spec, tok_spec), out_specs=(tok_spec, tok_spec, tok_spec, grad_spec, grad_spec, grad_spec), check_vma=False)
```

profile of v0, /device:TPU:97, one launch (start us, length us, event | category | flops | bytes accessed | tf_op | source)
XLA Modules:
  0.0 1723.3 jit_solution(5870688666640157237)
XLA Ops:
  1.7 14.7 scatter_custom_fusion
  40.5 16.4 subtract_add_fusion
  65.1 35.4 %gather_fusion.1 = bf16[8192,1024]{1,0:T(8,128)(2,1)} fusion(bf16[256,1024]{1,0:T(8,128)(2,1)S(1)} %copy-done.1, s32[8192]{0:T(1024)S(1)} %get-tuple-element.41), kind=kCustom, calls=%fused_computation.1 | custom fusion | bytes 33587200 | tf_op jit(solution)/shard_map/gather | solution.py:81
  100.5 13.9 copy.36
  123.0 45.5 %gather_fusion.3 = f32[8192]{0:T(1024)S(1)} fusion(f32[2048]{0:T(1024)S(1)} %reshape.220, s32[8192]{0:T(1024)S(1)} %get-tuple-element.40), kind=kCustom, calls=%fused_computation.3 | custom fusion | bytes 98304 | tf_op jit(solution)/shard_map/gather | solution.py:87
  168.6 35.4 %gather_fusion.4 = bf16[8192,1024]{1,0:T(8,128)(2,1)} fusion(bf16[256,1024]{1,0:T(8,128)(2,1)S(1)} %copy-done.2, s32[8192]{0:T(1024)S(1)} %get-tuple-element.41), kind=kCustom, calls=%fused_computation.4 | custom fusion | bytes 33587200 | tf_op jit(solution)/shard_map/gather | solution.py:88
  203.9 14.6 fusion
  218.6 87.1 %all-to-all-done = bf16[1,4,8,256,1024]{4,3,1,0,2:T(8,128)(2,1)} async-done(((bf16[1,4,8,256,1024]{4,3,1,0,2:T(8,128)(2,1)}), bf16[1,4,8,256,1024]{4,3,1,0,2:T(8,128)(2,1)}, u32[]{:S(2)}, u32[]{:S(2)}) %all-to-all-start) | async-done | bytes 16777248 | tf_op jit(solution)/shard_map/all_to_all | solution.py:50
  312.4 13.8 copy.37
  326.2 169.6 %all-to-all-done.4 = bf16[1,4,8,256,1024]{4,3,1,0,2:T(8,128)(2,1)} async-done(((bf16[1,4,8,256,1024]{4,3,1,0,2:T(8,128)(2,1)}), bf16[1,4,8,256,1024]{4,3,1,0,2:T(8,128)(2,1)}, u32[]{:S(2)}, u32[]{:S(2)}) %all-to-all-start.4) | async-done | bytes 16777248 | tf_op jit(solution)/shard_map/all_to_all | solution.py:50
  503.0 13.9 copy.44
  516.9 169.3 %all-to-all-done.1 = bf16[1,4,8,256,1024]{4,3,2,0,1:T(8,128)(2,1)} async-done(((bf16[1,4,8,256,1024]{4,3,2,0,1:T(8,128)(2,1)}), bf16[1,4,8,256,1024]{4,3,2,0,1:T(8,128)(2,1)}, u32[]{:S(2)}, u32[]{:S(2)}) %all-to-all-start.1) | async-done | bytes 16777248 | tf_op jit(solution)/shard_map/all_to_all | solution.py:51
  693.6 16.0 fusion.8
  709.6 15.7 fusion.12
  725.3 150.1 %all-to-all-done.5 = bf16[1,4,8,256,1024]{4,3,2,0,1:T(8,128)(2,1)} async-done(((bf16[1,4,8,256,1024]{4,3,2,0,1:T(8,128)(2,1)}), bf16[1,4,8,256,1024]{4,3,2,0,1:T(8,128)(2,1)}, u32[]{:S(2)}, u32[]{:S(2)}) %all-to-all-start.5) | async-done | bytes 16777248 | tf_op jit(solution)/shard_map/all_to_all | solution.py:51
  875.4 33.6 %multiply_convert_fusion = (bf16[8192,512]{1,0:T(8,128)(2,1)}, bf16[8192,512]{1,0:T(8,128)(2,1)}, bf16[8192,512]{1,0:T(8,128)(2,1)}) fusion(f32[8192,512]{1,0:T(8,128)} %fusion.12, f32[8192,512]{1,0:T(8,128)} %fusion.8, bf16[8192,1024]{1,0:T(8,128)(2,1)} %bitcast.47, bf16[1,512,1024]{2,1,0:T(8,128)(2,1)S(1)} %copy-done), kind=kOutput, calls=%fused_computation.12 | convolution fusion | flops 8652849152 | bytes 76546048 | tf_op jit(solution)/shard_map/ecd,efd->ecf/dot_general | solution.py:38
  909.0 15.9 convolution_convert_fusion
  932.1 18.8 %fusion.10 = f32[8192,1024]{1,0:T(8,128)} fusion(bf16[8192,512]{1,0:T(8,128)(2,1)} %get-tuple-element.38, bf16[1,1024,512]{2,1,0:T(8,128)(2,1)S(1)} %copy-done.7), kind=kOutput, calls=%fused_computation.31 | convolution fusion | flops 8589934592 | bytes 42991616 | tf_op jit(solution)/shard_map/ecf,edf->ecd/dot_general | solution.py:43
  950.9 23.1 %add_convert_fusion = bf16[8192,1024]{1,0:T(8,128)(2,1)} fusion(f32[8192,1024]{1,0:T(8,128)} %fusion.10, bf16[8192,512]{1,0:T(8,128)(2,1)} %get-tuple-element.37, bf16[1,1024,512]{2,1,0:T(8,128)(2,1)} %param.11), kind=kOutput, calls=%fused_computation.11 | convolution fusion | flops 8606711808 | bytes 59768832 | tf_op jit(solution)/shard_map/ecf,edf->ecd/dot_general | solution.py:43
  974.0 138.9 %all-to-all-done.2 = bf16[1,4,8,256,1024]{4,3,2,0,1:T(8,128)(2,1)} async-done(((bf16[1,4,8,256,1024]{4,3,2,0,1:T(8,128)(2,1)}), bf16[1,4,8,256,1024]{4,3,2,0,1:T(8,128)(2,1)}, u32[]{:S(2)}, u32[]{:S(2)}) %all-to-all-start.2) | async-done | bytes 16777248 | tf_op jit(solution)/shard_map/all_to_all | solution.py:58
  1120.0 13.9 copy.39
  1133.8 165.9 %all-to-all-done.6 = bf16[1,4,8,256,1024]{4,3,2,0,1:T(8,128)(2,1)} async-done(((bf16[1,4,8,256,1024]{4,3,2,0,1:T(8,128)(2,1)}), bf16[1,4,8,256,1024]{4,3,2,0,1:T(8,128)(2,1)}, u32[]{:S(2)}, u32[]{:S(2)}) %all-to-all-start.6) | async-done | bytes 16777248 | tf_op jit(solution)/shard_map/all_to_all | solution.py:58
  1310.1 13.9 copy.46
  1323.9 169.6 %all-to-all-done.3 = bf16[1,4,8,256,1024]{4,3,1,0,2:T(8,128)(2,1)} async-done(((bf16[1,4,8,256,1024]{4,3,1,0,2:T(8,128)(2,1)}), bf16[1,4,8,256,1024]{4,3,1,0,2:T(8,128)(2,1)}, u32[]{:S(2)}, u32[]{:S(2)}) %all-to-all-start.3) | async-done | bytes 16777248 | tf_op jit(solution)/shard_map/all_to_all | solution.py:59
  1508.5 16.1 convolution_bitcast_fusion
  1524.6 15.9 convolution_bitcast_fusion.1
  1540.6 13.4 convolution_bitcast_fusion.2
  1553.9 13.9 copy.40
  1567.8 19.2 %gather_fusion.2 = bf16[2048,1024]{1,0:T(8,128)(2,1)} fusion(bf16[8192,1024]{1,0:T(8,128)(2,1)} %bitcast.97, s32[2048]{0:T(1024)S(1)} %fusion.21), kind=kCustom, calls=%fused_computation.2 | custom fusion | bytes 8396800 | tf_op jit(solution)/shard_map/gather | solution.py:84
  1598.1 85.6 %all-to-all-done.7 = bf16[1,4,8,256,1024]{4,3,1,0,2:T(8,128)(2,1)} async-done(((bf16[1,4,8,256,1024]{4,3,1,0,2:T(8,128)(2,1)}), bf16[1,4,8,256,1024]{4,3,1,0,2:T(8,128)(2,1)}, u32[]{:S(2)}, u32[]{:S(2)}) %all-to-all-start.7) | async-done | bytes 16777248 | tf_op jit(solution)/shard_map/all_to_all | solution.py:59
  1683.8 13.9 copy.47
  1697.6 18.9 %gather_fusion.5 = bf16[2048,1024]{1,0:T(8,128)(2,1)} fusion(bf16[8192,1024]{1,0:T(8,128)(2,1)} %bitcast.96, s32[2048]{0:T(1024)S(1)} %fusion.21), kind=kCustom, calls=%fused_computation.5 | custom fusion | bytes 8396800 | tf_op jit(solution)/shard_map/gather | solution.py:92
  (58 shorter events, 120.2 us)
Async XLA Ops:
  0.6 874.7 %copy-start = (bf16[1,512,1024]{2,1,0:T(8,128)(2,1)S(1)}, bf16[1,512,1024]{2,1,0:T(8,128)(2,1)}, u32[]{:S(2)}) copy-start(bf16[1,512,1024]{2,1,0:T(8,128)(2,1)} %param.12) | copy-start | bytes 3145732
  0.6 64.4 %copy-start.1 = (bf16[256,1024]{1,0:T(8,128)(2,1)S(1)}, bf16[256,1024]{1,0:T(8,128)(2,1)}, u32[]{:S(2)}) copy-start(bf16[256,1024]{1,0:T(8,128)(2,1)} %param.7) | copy-start | bytes 1572868
  114.4 7.8 copy-start.6
  114.4 191.3 %all-to-all-start = ((bf16[1,4,8,256,1024]{4,3,1,0,2:T(8,128)(2,1)}), bf16[1,4,8,256,1024]{4,3,1,0,2:T(8,128)(2,1)}, u32[]{:S(2)}, u32[]{:S(2)}) async-start(bf16[1,4,8,256,1024]{4,3,1,0,2:T(8,128)(2,1)} %copy.36), calls=%async_computation | async-start | bytes 33554432 | tf_op jit(solution)/shard_map/all_to_all | solution.py:50
  122.3 0.7 copy-start.4
  123.0 45.6 %copy-start.2 = (bf16[256,1024]{1,0:T(8,128)(2,1)S(1)}, bf16[256,1024]{1,0:T(8,128)(2,1)}, u32[]{:S(2)}) copy-start(bf16[256,1024]{1,0:T(8,128)(2,1)} %param.13) | copy-start | bytes 1572868
  305.7 190.2 %all-to-all-start.4 = ((bf16[1,4,8,256,1024]{4,3,1,0,2:T(8,128)(2,1)}), bf16[1,4,8,256,1024]{4,3,1,0,2:T(8,128)(2,1)}, u32[]{:S(2)}, u32[]{:S(2)}) async-start(bf16[1,4,8,256,1024]{4,3,1,0,2:T(8,128)(2,1)} %fusion), calls=%async_computation.4 | async-start | bytes 33554432 | tf_op jit(solution)/shard_map/all_to_all | solution.py:50
  495.9 190.4 %all-to-all-start.1 = ((bf16[1,4,8,256,1024]{4,3,2,0,1:T(8,128)(2,1)}), bf16[1,4,8,256,1024]{4,3,2,0,1:T(8,128)(2,1)}, u32[]{:S(2)}, u32[]{:S(2)}) async-start(bf16[1,4,8,256,1024]{4,3,2,0,1:T(8,128)(2,1)} %copy.37), calls=%async_computation.1 | async-start | bytes 33554432 | tf_op jit(solution)/shard_map/all_to_all | solution.py:51
  686.2 189.1 %all-to-all-start.5 = ((bf16[1,4,8,256,1024]{4,3,2,0,1:T(8,128)(2,1)}), bf16[1,4,8,256,1024]{4,3,2,0,1:T(8,128)(2,1)}, u32[]{:S(2)}, u32[]{:S(2)}) async-start(bf16[1,4,8,256,1024]{4,3,2,0,1:T(8,128)(2,1)} %copy.44), calls=%async_computation.5 | async-start | bytes 33554432 | tf_op jit(solution)/shard_map/all_to_all | solution.py:51
  693.6 16.0 copy-start.7
  924.9 188.0 %all-to-all-start.2 = ((bf16[1,4,8,256,1024]{4,3,2,0,1:T(8,128)(2,1)}), bf16[1,4,8,256,1024]{4,3,2,0,1:T(8,128)(2,1)}, u32[]{:S(2)}, u32[]{:S(2)}) async-start(bf16[1,4,8,256,1024]{4,3,2,0,1:T(8,128)(2,1)} %bitcast.101), calls=%async_computation.2 | async-start | bytes 33554432 | tf_op jit(solution)/shard_map/all_to_all | solution.py:58
  1112.9 186.9 %all-to-all-start.6 = ((bf16[1,4,8,256,1024]{4,3,2,0,1:T(8,128)(2,1)}), bf16[1,4,8,256,1024]{4,3,2,0,1:T(8,128)(2,1)}, u32[]{:S(2)}, u32[]{:S(2)}) async-start(bf16[1,4,8,256,1024]{4,3,2,0,1:T(8,128)(2,1)} %bitcast.100), calls=%async_computation.6 | async-start | bytes 33554432 | tf_op jit(solution)/shard_map/all_to_all | solution.py:58
  1299.8 193.8 %all-to-all-start.3 = ((bf16[1,4,8,256,1024]{4,3,1,0,2:T(8,128)(2,1)}), bf16[1,4,8,256,1024]{4,3,1,0,2:T(8,128)(2,1)}, u32[]{:S(2)}, u32[]{:S(2)}) async-start(bf16[1,4,8,256,1024]{4,3,1,0,2:T(8,128)(2,1)} %copy.39), calls=%async_computation.3 | async-start | bytes 33554432 | tf_op jit(solution)/shard_map/all_to_all | solution.py:59
  1493.6 190.2 %all-to-all-start.7 = ((bf16[1,4,8,256,1024]{4,3,1,0,2:T(8,128)(2,1)}), bf16[1,4,8,256,1024]{4,3,1,0,2:T(8,128)(2,1)}, u32[]{:S(2)}, u32[]{:S(2)}) async-start(bf16[1,4,8,256,1024]{4,3,1,0,2:T(8,128)(2,1)} %copy.46), calls=%async_computation.7 | async-start | bytes 33554432 | tf_op jit(solution)/shard_map/all_to_all | solution.py:59
  1508.5 32.1 %slice-start = ((s8[8388608]{0:T(1024)(128)(4,1)}), s8[4194304]{0:T(1024)(128)(4,1)S(1)}, s32[]{:S(2)}) async-start(s8[8388608]{0:T(1024)(128)(4,1)} %bitcast.109), calls=%async_computation.8 | async-start | bytes 8388608
  1524.6 15.9 slice-start.1
  1567.8 19.2 %copy-start.3 = (bf16[256,1024]{1,0:T(8,128)(2,1)S(1)}, bf16[256,1024]{1,0:T(8,128)(2,1)}, u32[]{:S(2)}) copy-start(bf16[256,1024]{1,0:T(8,128)(2,1)} %param.13) | copy-start | bytes 1572868
  1567.8 24.7 %copy-start.5 = (f32[256,8]{1,0:T(8,128)S(1)}, f32[256,8]{1,0:T(8,128)}, u32[]{:S(2)}) copy-start(f32[256,8]{1,0:T(8,128)} %copy-done.4) | copy-start | bytes 24580
where the time goes:
time: 1730 us; the launch traced here: 1720 us
  waiting for transfers between devices  1140 us (66%)
  local copies, waits for them, and re-layouts  284 us (16%)
  matrix products  173 us (10%)
  other arithmetic  68.5 us (4%)
  starting transfers between devices  60.4 us (3%)
    all_to_all x2, waiting for transfers between devices, to_experts(): buffer = lax.all_to_all(buffer, 'ei', 1, 1, tiled=True)  319 us
    all_to_all x2, waiting for transfers between devices, to_tokens(): buffer = lax.all_to_all(buffer, 'ei', 1, 1, tiled=True)  305 us
    all_to_all x2, waiting for transfers between devices, to_experts(): buffer = lax.all_to_all(buffer, 'eo', 2, 2, tiled=True)  257 us
    all_to_all x2, waiting for transfers between devices, to_tokens(): buffer = lax.all_to_all(buffer, 'eo', 2, 2, tiled=True)  255 us
    gather x1, local copies, waits for them, and re-layouts, device_layer(): gate_loc.reshape(tok_count * top_k)[safe_owner]  45.5 us
    gather x1, local copies, waits for them, and re-layouts, device_layer(): x_loc[tok_of_slot]  35.4 us
    gather x1, local copies, waits for them, and re-layouts, device_layer(): do_send = (slot_gate[:, None] * dy_loc[tok_of_slot]).astype(jnp.bfloat16)  35.4 us
  transfers between devices with their start and end apart: 8, of which 8 were waited for; matrix products, arithmetic and copies ran while one was open for 19% of the time, Pallas kernels for 0%

commit v1 on v0

v1 whole, which is shorter than its diff:
```python
import jax
import jax.numpy as jnp
from jax import lax
from jax.sharding import PartitionSpec as P

GROUP = ('ei', 'eo')


def solution(mesh):
    ei_size = mesh.shape['ei']
    eo_size = mesh.shape['eo']
    group_devs = ei_size * eo_size
    tok_spec = P(('dp', 'ei', 'eo'), None)
    weight_spec = P(('ei', 'eo'), None, None)
    grad_spec = P(('dp', 'ei', 'eo'), None, None)

    def dot(a, b, dims):
        return lax.dot_general(a, b, (dims, ((), ())), preferred_element_type=jnp.float32)

    def device_layer(x_loc, idx_loc, gate_loc, wg_loc, wu_loc, wd_loc, dy_loc):
        tok_count, top_k = idx_loc.shape
        wg, wu, wd = wg_loc[0], wu_loc[0], wd_loc[0]
        me = lax.axis_index(GROUP)
        hit = idx_loc[None, :, :] == jnp.arange(group_devs, dtype=jnp.int32)[:, None, None]
        gate_dense = jnp.sum(jnp.where(hit, gate_loc[None], 0.0), axis=2)
        gates = lax.all_to_all(gate_dense, GROUP, 0, 0, tiled=True)
        gates = gates.reshape(group_devs * tok_count, 1)
        x_all = lax.all_gather(x_loc, GROUP, axis=0, tiled=True)
        dy_all = lax.all_gather(dy_loc, GROUP, axis=0, tiled=True)
        a = dot(x_all, wg, ((1,), (0,)))
        b = dot(x_all, wu, ((1,), (0,)))
        s = jax.nn.sigmoid(a)
        h = (a * s * b).astype(jnp.bfloat16)
        o = dot(h, wd, ((1,), (0,))).astype(jnp.bfloat16)
        y_part = gates * o
        y_loc = lax.psum_scatter(y_part, GROUP, scatter_dimension=0, tiled=True).astype(jnp.bfloat16)
        dg = jnp.sum(dy_all.astype(jnp.float32) * o.astype(jnp.float32), axis=1)
        dg = lax.all_to_all(dg.reshape(group_devs, tok_count), GROUP, 0, 0, tiled=True)
        dgate_loc = jnp.sum(jnp.where(hit, dg[:, :, None], 0.0), axis=0)
        g = (gates * dy_all).astype(jnp.bfloat16)
        dw_down = dot(h, g, ((0,), (0,)))
        dh = dot(g, wd, ((1,), (1,)))
        da = (dh * b * s * (1.0 + a * (1.0 - s))).astype(jnp.bfloat16)
        db = (dh * (a * s)).astype(jnp.bfloat16)
        dx_rows = (dot(da, wg, ((1,), (1,))) + dot(db, wu, ((1,), (1,)))).astype(jnp.bfloat16)
        dx_loc = lax.psum_scatter(dx_rows.astype(jnp.float32), GROUP, scatter_dimension=0, tiled=True).astype(jnp.bfloat16)
        dw_gate = dot(x_all, da, ((0,), (0,)))
        dw_up = dot(x_all, db, ((0,), (0,)))
        return y_loc, dx_loc, dgate_loc, dw_gate[None], dw_up[None], dw_down[None]

    return jax.shard_map(device_layer, mesh=mesh, in_specs=(tok_spec, tok_spec, tok_spec, weight_spec, weight_spec, weight_spec, tok_spec), out_specs=(tok_spec, tok_spec, tok_spec, grad_spec, grad_spec, grad_spec), check_vma=False)
```

time: 1730 us -> 553 us (0.32)
  waiting for transfers between devices: 1140 us -> 300 us
  local copies, waits for them, and re-layouts: 284 us -> 6.74 us
  starting transfers between devices: 60.4 us -> 0.25 us
  other arithmetic: 68.5 us -> 22.8 us
  blocking collectives: 0 us -> 21.5 us
    all_to_all x8 -> x0, waiting for transfers between devices: 1140 us -> none  [the longest x2 319 us: to_experts(): buffer = lax.all_to_all(buffer, 'ei', 1, 1, tiled=True)]
    reduce_scatter x0 -> x2, waiting for transfers between devices: none -> 189 us  [the longest x1 158 us: device_layer(): lax.psum_scatter(dx_rows.astype(jnp.float32), GROUP, scatter_dimension=0,...]
    gather x8 -> x0, local copies, waits for them, and re-layouts: 168 us -> none  [the longest x1 45.5 us: device_layer(): gate_loc.reshape(tok_count * top_k)[safe_owner]]
    all_gather x0 -> x2, waiting for transfers between devices: none -> 110 us  [the longest x1 71.4 us: device_layer(): x_all = lax.all_gather(x_loc, GROUP, axis=0, tiled=True)]
    all_to_all x6 -> x1, local copies, waits for them, and re-layouts: 83.2 us -> 0.03 us  [device_layer(): gates = lax.all_to_all(gate_dense, GROUP, 0, 0, tiled=True)]
    all_to_all x8 -> x0, starting transfers between devices: 60.4 us -> none  [the longest x2 17 us: to_tokens(): buffer = lax.all_to_all(buffer, 'eo', 2, 2, tiled=True)]
    all_to_all x0 -> x2, blocking collectives: none -> 21.5 us  [the longest x1 11.9 us: device_layer(): lax.all_to_all(dg.reshape(group_devs, tok_count), GROUP, 0, 0, tiled=True)]
    mul x0 -> x1, other arithmetic: none -> 18.8 us  [device_layer(): y_part = gates * o]
  transfers between devices with their start and end apart: 8 -> 4, of which waited for: 8 -> 4; matrix products, arithmetic and copies ran while one was open for 19% -> 30% of each run, Pallas kernels for 0% -> 0%
where the time goes in v1:
time: 553 us; the launch traced here: 550 us
  waiting for transfers between devices  300 us (54%)
  matrix products  184 us (33%)
  other arithmetic  22.8 us (4%)
  blocking collectives  21.5 us (4%)
  between operations  14.3 us (3%)
  local copies, waits for them, and re-layouts  6.74 us (1%)
    dot_general x9, matrix products, dot(): lax.dot_general(a, b, (dims, ((), ())), preferred_element_type=jnp.float32)  184 us
    reduce_scatter x1, waiting for transfers between devices, device_layer(): lax.psum_scatter(dx_rows.astype(jnp.float32), GROUP, scatter_dimension=0,...  158 us
    all_gather x1, waiting for transfers between devices, device_layer(): x_all = lax.all_gather(x_loc, GROUP, axis=0, tiled=True)  71.4 us
    all_gather x1, waiting for transfers between devices, device_layer(): dy_all = lax.all_gather(dy_loc, GROUP, axis=0, tiled=True)  38.5 us
    reduce_scatter x1, waiting for transfers between devices, device_layer(): lax.psum_scatter(y_part, GROUP, scatter_dimension=0, tiled=True)  31.5 us
    mul x1, other arithmetic, device_layer(): y_part = gates * o  18.8 us
    all_to_all x1, blocking collectives, device_layer(): lax.all_to_all(dg.reshape(group_devs, tok_count), GROUP, 0, 0, tiled=True)  11.9 us
  transfers between devices with their start and end apart: 4, of which 4 were waited for; matrix products, arithmetic and copies ran while one was open for 30% of the time, Pallas kernels for 0%

profile of v1, /device:TPU:97, one launch (start us, length us, event | category | flops | bytes accessed | tf_op | source)
XLA Modules:
  0.0 549.8 jit_solution(9462778022022989750)
XLA Ops:
  7.2 0.0 copy-start
  7.2 0.1 all-gather.3.cloned.1.call-start
  7.3 0.7 all-gather.3.cloned.1.call-update
  8.0 0.1 all-gather.5.cloned.1.call-start
  8.1 2.0 copy.26
  10.1 0.1 all-gather.5.cloned.1.call-update
  10.2 0.1 reduce-scatter.3.cloned.1.call-start
  10.2 71.4 %all-gather.3.cloned.1.call-done = bf16[8192,1024]{1,0:T(8,128)(2,1)} async-done(((bf16[256,1024]{1,0:T(8,128)(2,1)}), bf16[8192,1024]{1,0:T(8,128)(2,1)}) %all-gather.3.cloned.1.call-update) | async-done | bytes 16777232 | tf_op jit(solution)/shard_map/all_gather | solution.py:28
  81.7 15.9 %fusion.18 = f32[8192,512]{1,0:T(8,128)} fusion(bf16[8192,1024]{1,0:T(8,128)(2,1)} %all-gather.3.cloned.1.call-done, bf16[1,1024,512]{2,1,0:T(8,128)(2,1)} %param.10), kind=kOutput, calls=%fused_computation.25 | convolution fusion | flops 8589934592 | bytes 34603008 | tf_op jit(solution)/shard_map/dot_general | solution.py:18
  97.6 21.6 %multiply_convert_fusion.2 = (bf16[8192,512]{1,0:T(8,128)(2,1)}, f32[8192,512]{1,0:T(8,128)}) fusion(f32[8192,512]{1,0:T(8,128)} %fusion.18, bf16[8192,1024]{1,0:T(8,128)(2,1)} %all-gather.3.cloned.1.call-done, bf16[1,1024,512]{2,1,0:T(8,128)(2,1)S(1)} %copy-done.2), kind=kOutput, calls=%fused_computation.9 | convolution fusion | flops 8615100416 | bytes 59768832 | tf_op jit(solution)/shard_map/dot_general | solution.py:18
  119.1 38.5 %all-gather.5.cloned.1.call-done = bf16[8192,1024]{0,1:T(8,128)(2,1)} async-done(((bf16[256,1024]{0,1:T(8,128)(2,1)}), bf16[8192,1024]{0,1:T(8,128)(2,1)}) %all-gather.5.cloned.1.call-update) | async-done | bytes 16777232 | tf_op jit(solution)/shard_map/all_gather | solution.py:29
  157.7 28.4 %fusion.1 = (f32[8192]{0:T(1024)S(1)}, bf16[8192,1024]{0,1:T(8,128)(2,1)}) fusion(bf16[8192,1024]{0,1:T(8,128)(2,1)} %all-gather.5.cloned.1.call-done, bf16[8192,512]{1,0:T(8,128)(2,1)} %get-tuple-element.28, bf16[1,512,1024]{2,1,0:T(8,128)(2,1)S(1)} %copy-done), kind=kOutput, calls=%fused_computation.4 | convolution fusion | flops 8631869440 | bytes 43024384 | tf_op jit(solution)/shard_map/dot_general | solution.py:18
  186.0 11.9 %all_to_all.18 = f32[32,1,256]{2,1,0:T(1,128)S(1)} all-to-all(f32[32,1,256]{2,1,0:T(1,128)S(1)} %bitcast.52), channel_id=1, replica_groups=mesh['dp'=1,'ei'=4,'eo'=8] {'ei','eo'}, dimensions={0} | all-to-all | bytes 65536 | tf_op jit(solution)/shard_map/all_to_all | solution.py:38
  197.9 0.7 select_reduce_fusion
  198.6 9.6 %all_to_all.19 = f32[32,1,256]{2,1,0:T(1,128)S(1)} all-to-all(f32[32,1,256]{2,1,0:T(1,128)S(1)} %copy.25), channel_id=1, replica_groups=mesh['dp'=1,'ei'=4,'eo'=8] {'ei','eo'}, dimensions={0} | all-to-all | bytes 65536 | tf_op jit(solution)/shard_map/all_to_all | solution.py:26
  208.3 18.8 %convert_multiply_fusion.2 = f32[8192,1024]{0,1:T(8,128)} fusion(bf16[8192,1024]{0,1:T(8,128)(2,1)} %get-tuple-element.31, f32[8192]{0:T(1024)S(1)} %bitcast.49), kind=kLoop, calls=%fused_computation.2 | loop fusion | flops 16777216 | bytes 50364416 | tf_op jit(solution)/shard_map/mul | solution.py:35
  227.1 0.1 reduce-scatter.3.cloned.1.call-update
  227.1 0.1 reduce-scatter.5.cloned.1.call-start
  227.2 29.1 %multiply_convert_fusion = (bf16[8192,512]{1,0:T(8,128)(2,1)}, bf16[8192,512]{1,0:T(8,128)(2,1)}) fusion(f32[8192,512]{1,0:T(8,128)} %fusion.18, f32[8192,512]{1,0:T(8,128)} %get-tuple-element.29, bf16[1,512,1024]{2,1,0:T(8,128)(2,1)S(1)} %copy-done, bf16[8192,1024]{0,1:T(8,128)(2,1)} %all-gather.5.cloned.1.call-done, f32[8192]{0:T(1024)S(1)} %bitcast.50), kind=kOutput, calls=%fused_computation.7 | convolution fusion | flops 8669626368 | bytes 68190208 | tf_op jit(solution)/shard_map/dot_general | solution.py:18
  256.3 18.8 %fusion.16 = f32[8192,1024]{1,0:T(8,128)} fusion(bf16[8192,512]{1,0:T(8,128)(2,1)} %get-tuple-element.27, bf16[1,1024,512]{2,1,0:T(8,128)(2,1)S(1)} %copy-done.5), kind=kOutput, calls=%fused_computation.23 | convolution fusion | flops 8589934592 | bytes 42991616 | tf_op jit(solution)/shard_map/dot_general | solution.py:18
  275.1 25.6 %fusion.2 = f32[8192,1024]{1,0:T(8,128)} fusion(f32[8192,1024]{1,0:T(8,128)} %fusion.16, bf16[8192,512]{1,0:T(8,128)(2,1)} %get-tuple-element.26, bf16[1,1024,512]{2,1,0:T(8,128)(2,1)S(1)} %copy-done.2), kind=kOutput, calls=%fused_computation.6 | convolution fusion | flops 8615100416 | bytes 76546048 | tf_op jit(solution)/shard_map/dot_general | solution.py:18
  300.7 0.1 reduce-scatter.5.cloned.1.call-update
  300.7 14.4 %convolution_bitcast_fusion.1 = f32[1,1024,512]{1,2,0:T(8,128)S(1)} fusion(bf16[8192,512]{1,0:T(8,128)(2,1)} %get-tuple-element.27, bf16[8192,1024]{1,0:T(8,128)(2,1)} %all-gather.3.cloned.1.call-done), kind=kOutput, calls=%fused_computation.17 | convolution fusion | flops 8589934592 | bytes 27262976 | tf_op jit(solution)/shard_map/dot_general | solution.py:18
  315.1 1.8 copy.28
  316.9 14.4 %convolution_bitcast_fusion = f32[1,1024,512]{1,2,0:T(8,128)S(1)} fusion(bf16[8192,512]{1,0:T(8,128)(2,1)} %get-tuple-element.26, bf16[8192,1024]{1,0:T(8,128)(2,1)} %all-gather.3.cloned.1.call-done), kind=kOutput, calls=%fused_computation.16 | convolution fusion | flops 8589934592 | bytes 27262976 | tf_op jit(solution)/shard_map/dot_general | solution.py:18
  331.3 1.8 copy.29
  333.2 16.1 %fusion.8 = f32[1,512,1024]{2,1,0:T(8,128)} fusion(bf16[8192,512]{1,0:T(8,128)(2,1)} %get-tuple-element.28, bf16[8192,1024]{0,1:T(8,128)(2,1)} %all-gather.5.cloned.1.call-done, f32[8192]{0:T(1024)S(1)} %bitcast.51), kind=kOutput, calls=%fused_computation.15 | convolution fusion | flops 8615100416 | bytes 27295744 | tf_op jit(solution)/shard_map/dot_general | solution.py:18
  349.3 31.5 %reduce-scatter.3.cloned.1.call-done = f32[256,1024]{0,1:T(8,128)} async-done(((f32[8192,1024]{0,1:T(8,128)}), f32[256,1024]{0,1:T(8,128)}) %reduce-scatter.3.cloned.1.call-update) | async-done | bytes 1048592 | tf_op jit(solution)/shard_map/reduce_scatter | solution.py:36
  380.8 1.3 convert_element_type.38
  382.1 1.0 copy.27
  383.1 157.6 %reduce-scatter.5.cloned.1.call-done = f32[256,1024]{1,0:T(8,128)} async-done(((f32[8192,1024]{1,0:T(8,128)}), f32[256,1024]{1,0:T(8,128)}) %reduce-scatter.5.cloned.1.call-update) | async-done | bytes 1048592 | tf_op jit(solution)/shard_map/reduce_scatter | solution.py:46
  540.7 2.1 convert_element_type.45
  (13 shorter events, 0.1 us)
Async XLA Ops:
  7.2 150.5 %copy-start = (bf16[1,512,1024]{2,1,0:T(8,128)(2,1)S(1)}, bf16[1,512,1024]{2,1,0:T(8,128)(2,1)}, u32[]{:S(2)}) copy-start(bf16[1,512,1024]{2,1,0:T(8,128)(2,1)} %param.12) | copy-start | bytes 3145732
  7.2 74.5 %all-gather.3.cloned.1.call-start = ((), (), s32[]{:S(2)}) async-start(), calls=%async_computation.4 | async-start | bytes 17301504 | tf_op jit(solution)/shard_map/all_gather | solution.py:28
  8.0 149.7 %all-gather.5.cloned.1.call-start = ((), (), s32[]{:S(2)}) async-start(), calls=%async_computation.6 | async-start | bytes 17301504 | tf_op jit(solution)/shard_map/all_gather | solution.py:29
  10.2 87.4 %copy-start.2 = (bf16[1,1024,512]{2,1,0:T(8,128)(2,1)S(1)}, bf16[1,1024,512]{2,1,0:T(8,128)(2,1)}, u32[]{:S(2)}) copy-start(bf16[1,1024,512]{2,1,0:T(8,128)(2,1)} %param.11) | copy-start | bytes 3145732
  10.2 370.7 %reduce-scatter.3.cloned.1.call-start = ((), (), s32[]{:S(2)}) async-start(), calls=%async_computation.5 | async-start | bytes 34603008 | tf_op jit(solution)/shard_map/reduce_scatter | solution.py:36
  157.7 40.3 %copy-start.3 = (s32[256,8]{0,1:T(8,128)S(1)}, s32[256,8]{0,1:T(8,128)}, u32[]{:S(2)}) copy-start(s32[256,8]{0,1:T(8,128)} %param.8) | copy-start | bytes 24580
  157.7 40.3 %copy-start.4 = (f32[256,8]{0,1:T(8,128)S(1)}, f32[256,8]{0,1:T(8,128)}, u32[]{:S(2)}) copy-start(f32[256,8]{0,1:T(8,128)} %param.9) | copy-start | bytes 24580
  227.1 313.6 %reduce-scatter.5.cloned.1.call-start = ((), (), s32[]{:S(2)}) async-start(), calls=%async_computation.7 | async-start | bytes 34603008 | tf_op jit(solution)/shard_map/reduce_scatter | solution.py:46
  227.2 29.1 %copy-start.5 = (bf16[1,1024,512]{2,1,0:T(8,128)(2,1)S(1)}, bf16[1,1024,512]{2,1,0:T(8,128)(2,1)}, u32[]{:S(2)}) copy-start(bf16[1,1024,512]{2,1,0:T(8,128)(2,1)} %param.10) | copy-start | bytes 3145732
  333.2 209.7 %copy-start.1 = (bf16[1,512,1024]{2,1,0:T(8,128)(2,1)S(1)}, bf16[1,512,1024]{2,1,0:T(8,128)(2,1)}, u32[]{:S(2)}) copy-start(bf16[1,512,1024]{2,1,0:T(8,128)(2,1)} %param.12) | copy-start | bytes 3145732
Sparse Core Ops, SparseCore 0:
  10.1 71.5 all-gather.2
  84.2 73.3 all-gather.4
  227.3 153.5 reduce-scatter.2
  384.4 156.2 reduce-scatter.4

commit v2 on v1

v2 whole, which is shorter than its diff:
```python
import functools

import jax
import jax.numpy as jnp
from jax import lax
from jax.experimental import pallas as pl
from jax.experimental.pallas import tpu as pltpu
from jax.sharding import PartitionSpec as P

MESH = pl.DeviceIdType.MESH
RINGS = 4
CORES = 2
SLOTS = 4
LANES = 128
F32 = jnp.float32
BF16 = jnp.bfloat16


def dot(a, b, dim_a, dim_b):
    return lax.dot_general(a, b, (((dim_a,), (dim_b,)), ((), ())), preferred_element_type=F32)


def kernel(nx, ny, x_hbm, dy_hbm, gt_hbm, wg_hbm, wu_hbm, wd_hbm,
           y_out, dx_out, dgt_out, dwg_out, dwu_out, dwd_out,
           xy, gt, acc, accg, con, cong, wg, wu, wd, dwg, dwu, dwd, rwg, rwu, rwd,
           loc_sem, xs, xr, gs, gr, acs, acr, ags, agr, ws, wr, ds, dr, free_x, free_a):
    steps = nx * ny
    dp = lax.axis_index('dp')
    row = lax.axis_index('ei')
    eo = lax.axis_index('eo')
    col, core = eo // CORES, eo % CORES
    experts = steps * CORES
    expert_ids = (row * nx * CORES + eo, row * nx * CORES + col * CORES + (1 - core))

    def dev(c, r):
        return (dp, (r + ny) % ny, ((c + nx) % nx) * CORES + core)

    turn = ((col + row) % nx) // (nx - 1)
    back = ((col + row + nx - 1) % nx) // (nx - 1)
    up_a, dn_a = dev(col + 1 - turn, row + turn), dev(col - 1 + back, row - back)
    up_b, dn_b = dev(col + turn, row + 1 - turn), dev(col - back, row - 1 + back)
    nxt = (up_a, dn_a, up_b, dn_b)
    prv = (dn_a, up_a, dn_b, up_b)
    mate = (dp, row, col * CORES + (1 - core))

    loads = [pltpu.make_async_copy(s, d, loc_sem.at[i]) for i, (s, d) in enumerate((
        (x_hbm, xy.at[0, 0]), (dy_hbm, xy.at[0, 1]), (gt_hbm, gt.at[0]),
        (wg_hbm, wg.at[0]), (wu_hbm, wu.at[0]), (wd_hbm, wd.at[0])))]
    for load in loads:
        load.start()

    barrier = pltpu.get_barrier_semaphore()
    for peer in nxt + (mate,):
        pl.semaphore_signal(barrier, inc=1, device_id=peer, device_id_type=MESH)
    pl.semaphore_wait(barrier, RINGS + 1)

    def remote(src, dst, send, recv, peer):
        return pltpu.make_async_remote_copy(src_ref=src, dst_ref=dst, send_sem=send, recv_sem=recv, device_id=peer, device_id_type=MESH)

    weights = [remote(s, d.at[1], ws.at[i], wr.at[i], mate) for i, (s, d) in enumerate(((wg_hbm, wg), (wu_hbm, wu), (wd_hbm, wd)))]
    grads = [remote(s.at[1], d, ds.at[i], dr.at[i], mate) for i, (s, d) in enumerate(((dwg, rwg), (dwu, rwu), (dwd, rwd)))]

    def fwd(s, r):
        a, b = s % SLOTS, (s + 1) % SLOTS
        return (remote(xy.at[a, :, r], xy.at[b, :, r], xs.at[a, r], xr.at[b, r], nxt[r]),
                remote(gt.at[a, r], gt.at[b, r], gs.at[a, r], gr.at[b, r], nxt[r]))

    def push(s, k, r):
        a, b = s % SLOTS, (s + 1) % SLOTS
        return remote(acc.at[a, k, r], acc.at[b, k, r], acs.at[a, k, r], acr.at[b, k, r], nxt[r])

    def pushg(s, r):
        a, b = s % SLOTS, (s + 1) % SLOTS
        return remote(accg.at[a, r], accg.at[b, r], ags.at[a, r], agr.at[b, r], nxt[r])

    for load in loads[:3]:
        load.wait()
    for r in range(RINGS):
        for c in fwd(0, r):
            c.start()
    for w in weights:
        w.start()
    for ref in (dwg, dwu, dwd):
        ref[...] = jnp.zeros_like(ref)
    for load in loads[3:]:
        load.wait()

    tr = xy.shape[3]
    d_model = xy.shape[4]
    tok = RINGS * tr
    groups = LANES // experts
    pk = tr // groups
    lane = lax.broadcasted_iota(jnp.int32, (pk, LANES), 1)

    def compute(s):
        slot = s % SLOTS
        which = jnp.minimum(s, 1)
        for e in range(CORES):
            if e == 1:
                @pl.when(s == 0)
                def _():
                    for w in weights:
                        w.wait()
            gate = jnp.concatenate([
                jnp.sum(jnp.where(lane == q * experts + expert_ids[e], gt[slot, r], 0.0), axis=1, keepdims=True)
                for r in range(RINGS) for q in range(groups)], axis=0)
            x = xy[slot, 0].reshape(tok, d_model)
            dy = xy[slot, 1].reshape(tok, d_model)
            xm = x * jnp.where(gate > 0.0, 1.0, 0.0).astype(BF16)
            a = dot(xm, wg[e], 1, 0)
            b = dot(xm, wu[e], 1, 0)
            sig = jax.nn.sigmoid(a)
            silu = a * sig
            h = (silu * b).astype(BF16)
            o = dot(h, wd[e], 1, 0).astype(BF16).astype(F32)
            dy32 = dy.astype(F32)
            dg = jnp.sum(dy32 * o, axis=1, keepdims=True)
            g32 = gate * dy32
            g = g32.astype(BF16)
            yc = (gate * o).reshape(RINGS, tr, d_model)
            packed = [functools.reduce(lambda p, v: p + v, [
                jnp.where(lane == q * experts + expert_ids[e], dg[(r * groups + q) * pk:(r * groups + q + 1) * pk], 0.0)
                for q in range(groups)]) for r in range(RINGS)]
            if e == 0:
                con[which, 0] = yc
                for r in range(RINGS):
                    cong[which, r] = packed[r]
            else:
                con[which, 0] += yc
                for r in range(RINGS):
                    cong[which, r] += packed[r]
            dwd[e] += dot(h, g, 0, 0)
            dh = dot(g, wd[e], 1, 1)
            da = (dh * b * sig * (1.0 + a * (1.0 - sig))).astype(BF16)
            db = (dh * silu).astype(BF16)
            dxc = (dot(da, wg[e], 1, 1) + dot(db, wu[e], 1, 1)).astype(BF16).astype(F32).reshape(RINGS, tr, d_model)
            if e == 0:
                con[which, 1] = dxc
            else:
                con[which, 1] += dxc
            dwg[e] += dot(x, da, 0, 0)
            dwu[e] += dot(x, db, 0, 0)

    def step(s, _):
        slot = s % SLOTS
        compute(s)

        @pl.when(s < steps - 1)
        def _():
            for r in range(RINGS):
                for c in fwd(s, r):
                    c.wait_recv()

        @pl.when(s < steps - 2)
        def _():
            for r in range(RINGS):
                @pl.when(s + 2 >= SLOTS)
                def _():
                    pl.semaphore_wait(free_x.at[r], 1)
                for c in fwd(s + 1, r):
                    c.start()

        @pl.when(s == steps - 1)
        def _():
            for c in grads:
                c.start()

        @pl.when(s >= 1)
        def _():
            for k in range(2):
                for r in range(RINGS):
                    @pl.when(s == 1)
                    def _():
                        acc[slot, k, r] = con[1, k, r]

                    @pl.when(s >= 2)
                    def _():
                        push(s - 1, k, r).wait_recv()
                        acc[slot, k, r] += con[1, k, r]
                    if k == 0:
                        @pl.when(s == 1)
                        def _():
                            accg[slot, r] = cong[1, r]

                        @pl.when(s >= 2)
                        def _():
                            pushg(s - 1, r).wait_recv()
                            accg[slot, r] += cong[1, r]
                for r in range(RINGS):
                    if k == 0:
                        @pl.when(s >= SLOTS)
                        def _():
                            pl.semaphore_wait(free_a.at[r], 1)
                    push(s, k, r).start()
                    if k == 1:
                        pushg(s, r).start()

        @pl.when((s >= 1) & (s <= steps - 1))
        def _():
            for r in range(RINGS):
                for c in fwd(s - 1, r):
                    c.wait_send()

                @pl.when(s <= steps - SLOTS)
                def _():
                    pl.semaphore_signal(free_x.at[r], inc=1, device_id=prv[r], device_id_type=MESH)

        @pl.when(s >= 2)
        def _():
            for r in range(RINGS):
                for k in range(2):
                    push(s - 1, k, r).wait_send()
                pushg(s - 1, r).wait_send()

                @pl.when(s - 1 <= steps - SLOTS)
                def _():
                    pl.semaphore_signal(free_a.at[r], inc=1, device_id=prv[r], device_id_type=MESH)
        return 0

    lax.fori_loop(0, steps, step, 0)

    home = steps % SLOTS
    for c in grads:
        c.wait()
    dwg_out[...] = dwg[0] + rwg[...]
    dwu_out[...] = dwu[0] + rwu[...]
    dwd_out[...] = dwd[0] + rwd[...]
    for r in range(RINGS):
        rows = pl.ds(r * tr, tr)
        for k, out in ((0, y_out), (1, dx_out)):
            push(steps - 1, k, r).wait()
            out[rows, :] = (acc[home, k, r] + con[0, k, r]).astype(BF16)
        pushg(steps - 1, r).wait()
        dgt_out[r] = accg[home, r] + cong[0, r]


def solution(mesh):
    ny = mesh.shape['ei']
    nx = mesh.shape['eo'] // CORES
    experts = ny * nx * CORES
    groups = LANES // experts
    tok_spec = P(('dp', 'ei', 'eo'), None)
    weight_spec = P(('ei', 'eo'), None, None)
    grad_spec = P(('dp', 'ei', 'eo'), None, None)
    hbm = pl.BlockSpec(memory_space=pl.ANY)
    vmem = pl.BlockSpec(memory_space=pltpu.VMEM)

    def device_layer(x_loc, idx_loc, gate_loc, wg_loc, wu_loc, wd_loc, dy_loc):
        tok, _ = idx_loc.shape
        d_model = x_loc.shape[1]
        d_ff = wg_loc.shape[2]
        tr = tok // RINGS
        pk = tr // groups
        hit = idx_loc[:, :, None] == jnp.arange(experts, dtype=jnp.int32)
        gates = jnp.sum(jnp.where(hit, gate_loc[:, :, None], 0.0), axis=1)
        gates = gates.reshape(RINGS, groups, pk, experts).transpose(0, 2, 1, 3).reshape(RINGS, pk, LANES)
        dma = pltpu.SemaphoreType.DMA
        steps = nx * ny
        row_bytes = tok * d_model
        y_loc, dx_loc, dgt, dwg, dwu, dwd = pl.pallas_call(
            functools.partial(kernel, nx, ny),
            out_shape=(
                jax.ShapeDtypeStruct((tok, d_model), BF16), jax.ShapeDtypeStruct((tok, d_model), BF16),
                jax.ShapeDtypeStruct((RINGS, pk, LANES), F32),
                jax.ShapeDtypeStruct((d_model, d_ff), F32), jax.ShapeDtypeStruct((d_model, d_ff), F32),
                jax.ShapeDtypeStruct((d_ff, d_model), F32)),
            in_specs=[hbm] * 6,
            out_specs=(vmem,) * 6,
            scratch_shapes=[
                pltpu.VMEM((SLOTS, 2, RINGS, tr, d_model), BF16),
                pltpu.VMEM((SLOTS, RINGS, pk, LANES), F32),
                pltpu.VMEM((SLOTS, 2, RINGS, tr, d_model), F32),
                pltpu.VMEM((SLOTS, RINGS, pk, LANES), F32),
                pltpu.VMEM((2, 2, RINGS, tr, d_model), F32),
                pltpu.VMEM((2, RINGS, pk, LANES), F32),
                pltpu.VMEM((CORES, d_model, d_ff), BF16), pltpu.VMEM((CORES, d_model, d_ff), BF16), pltpu.VMEM((CORES, d_ff, d_model), BF16),
                pltpu.VMEM((CORES, d_model, d_ff), F32), pltpu.VMEM((CORES, d_model, d_ff), F32), pltpu.VMEM((CORES, d_ff, d_model), F32),
                pltpu.VMEM((d_model, d_ff), F32), pltpu.VMEM((d_model, d_ff), F32), pltpu.VMEM((d_ff, d_model), F32),
                dma((6,)), dma((SLOTS, RINGS)), dma((SLOTS, RINGS)), dma((SLOTS, RINGS)), dma((SLOTS, RINGS)),
                dma((SLOTS, 2, RINGS)), dma((SLOTS, 2, RINGS)), dma((SLOTS, RINGS)), dma((SLOTS, RINGS)),
                dma((3,)), dma((3,)), dma((3,)), dma((3,)),
                pltpu.SemaphoreType.REGULAR((RINGS,)), pltpu.SemaphoreType.REGULAR((RINGS,)),
            ],
            compiler_params=pltpu.CompilerParams(collective_id=0, has_side_effects=True, vmem_limit_bytes=66000000),
            cost_estimate=pl.CostEstimate(flops=18 * steps * row_bytes * d_ff * CORES, bytes_accessed=steps * row_bytes * 12, transcendentals=0),
        )(x_loc.reshape(RINGS, tr, d_model), dy_loc.reshape(RINGS, tr, d_model), gates, wg_loc[0], wu_loc[0], wd_loc[0])
        dgt = dgt.reshape(RINGS, pk, groups, experts).transpose(0, 2, 1, 3).reshape(tok, experts)
        dgate_loc = jnp.sum(jnp.where(hit, dgt[:, None, :], 0.0), axis=2)
        return y_loc, dx_loc, dgate_loc, dwg[None], dwu[None], dwd[None]

    return jax.shard_map(device_layer, mesh=mesh, in_specs=(tok_spec, tok_spec, tok_spec, weight_spec, weight_spec, weight_spec, tok_spec), out_specs=(tok_spec, tok_spec, tok_spec, grad_spec, grad_spec, grad_spec), check_vma=False)
```

time: 553 us -> 293 us (0.53)
  waiting for transfers between devices: 300 us -> 0 us
  Pallas kernels: 0 us -> 279 us
  matrix products: 184 us -> 0 us
  blocking collectives: 21.5 us -> 0 us
  other arithmetic: 22.8 us -> 1.41 us
  between operations: 14.3 us -> 0.68 us
    pallas_call x0 -> x1, Pallas kernels: none -> 279 us  [device_layer(): pl.pallas_call(functools.partial(kernel, nx, ny), out_shape=(jax.ShapeDty...]
    reduce_scatter x2 -> x0, waiting for transfers between devices: 189 us -> none  [the longest x1 158 us: device_layer(): lax.psum_scatter(dx_rows.astype(jnp.float32), GROUP, scatter_dimension=0,...]
    dot_general x9 -> x0, matrix products: 184 us -> none  [dot(): lax.dot_general(a, b, (dims, ((), ())), preferred_element_type=jnp.float32)]
    all_gather x2 -> x0, waiting for transfers between devices: 110 us -> none  [the longest x1 71.4 us: device_layer(): x_all = lax.all_gather(x_loc, GROUP, axis=0, tiled=True)]
    all_to_all x2 -> x0, blocking collectives: 21.5 us -> none  [the longest x1 11.9 us: device_layer(): lax.all_to_all(dg.reshape(group_devs, tok_count), GROUP, 0, 0, tiled=True)]
    mul x1 -> x0, other arithmetic: 18.8 us -> none  [device_layer(): y_part = gates * o]
  transfers between devices with their start and end apart: 4 -> 0, of which waited for: 4 -> 0; matrix products, arithmetic and copies ran while one was open for 30% -> 0% of each run, Pallas kernels for 0% -> 0%
where the time goes in v2:
time: 293 us; the launch traced here: 292 us
  Pallas kernels  279 us (95%)
  local copies, waits for them, and re-layouts  11.7 us (4%)
    pallas_call x1, Pallas kernels, device_layer(): pl.pallas_call(functools.partial(kernel, nx, ny), out_shape=(jax.ShapeDty...  279 us
    unnamed x13, local copies, waits for them, and re-layouts  9.76 us

profile of v2, /device:TPU:97, one launch (start us, length us, event | category | flops | bytes accessed | tf_op | source)
XLA Modules:
  0.0 292.4 jit_solution(12358089215727448974)
XLA Ops:
  0.6 0.8 select_reduce_fusion.1
  1.4 0.1 copy.19
  1.5 0.1 copy.20
  1.5 0.7 reshape.33.gt_hbm
  2.3 0.0 copy-start.3
  2.3 278.5 %shard_map.118 = (bf16[256,1024]{1,0:T(8,128)(2,1)}, bf16[256,1024]{1,0:T(8,128)(2,1)}, f32[4,16,128]{2,1,0:T(8,128)}, f32[1024,512]{1,0:T(8,128)}, f32[1024,512]{1,0:T(8,128)}, /*index=5*/f32[512,1024]{1,0:T(8,128)}) custom-call(bf16[4,64,1024]{2,1,0:T(8,128)(2,1)} %bitcast.22, bf16[4,64,1024]{2,1,0:T(8,128)(2,1)} %bitcast.23, ...), custom_call_target="tpu_custom_call" | custom-call | flops 77309411328 | bytes 50331648 | tf_op jit(solution)/shard_map/pallas_call | solution.py:260
  280.8 0.0 copy-start.2
  280.8 1.0 reshape.34
  281.9 0.1 copy.22
  281.9 0.0 copy-done.3
  281.9 0.7 select_reduce_fusion
  282.6 1.9 copy.28
  284.5 1.9 copy.29
  286.3 0.0 copy-done.2
  286.3 0.0 copy-start.1
  286.3 1.3 copy.30
  287.7 1.0 copy-done.1
  288.7 0.0 copy-start
  288.7 1.3 copy.31
  290.0 1.0 copy-done
  291.0 1.3 copy.32
  (1 shorter events, 0.0 us)
Async XLA Ops:
  2.3 279.7 %copy-start.3 = (s32[256,8]{0,1:T(8,128)S(1)}, s32[256,8]{0,1:T(8,128)}, u32[]{:S(2)}) copy-start(s32[256,8]{0,1:T(8,128)} %param.8) | copy-start | bytes 24580
  280.8 5.5 %copy-start.2 = (f32[1024,512]{1,0:T(8,128)S(1)}, f32[1024,512]{1,0:T(8,128)}, u32[]{:S(2)}) copy-start(f32[1024,512]{1,0:T(8,128)} %get-tuple-element.15) | copy-start | bytes 6291460
  286.3 2.3 copy-start.1
  288.7 2.3 copy-start

commit v3 on v1

v3 whole, which is shorter than its diff:
```python
import functools

import jax
import jax.numpy as jnp
from jax import lax
from jax.experimental import pallas as pl
from jax.experimental.pallas import tpu as pltpu
from jax.sharding import PartitionSpec as P

MESH = pl.DeviceIdType.MESH
SIDE = 4
CORES = 2
LANES = 128
F32 = jnp.float32
BF16 = jnp.bfloat16
N_MSG = 96


def dot(a, b, dim_a, dim_b):
    return lax.dot_general(a, b, (((dim_a,), (dim_b,)), ((), ())), preferred_element_type=F32)


def kernel(x_hbm, dy_hbm, gt_hbm, wg_hbm, wu_hbm, wd_hbm,
           y_out, dx_out, dgt_out, dwg_out, dwu_out, dwd_out, whg, whu, whd,
           xyc, xyo, gtc, gto, con, cong, rsh, rshg, rsf, rsfg, wg, wu, wd, dwg, dwu, dwd,
           send_sem, recv_sem, loc_sem, wl_sem):
    dp = lax.axis_index('dp')
    row = lax.axis_index('ei')
    eo = lax.axis_index('eo')
    col, core = eo // CORES, eo % CORES
    experts = SIDE * SIDE * CORES

    def dev(c, r, k):
        return (dp, (r + SIDE) % SIDE, ((c + SIDE) % SIDE) * CORES + k)

    xpeer = (dev(col + 1, row, core), dev(col - 1, row, core))
    ypeer = (dev(col, row + 1, core), dev(col, row - 1, core))
    mate = dev(col, row, 1 - core)

    def expert_id(p, i):
        return row * SIDE * CORES + ((col + i) % SIDE) * CORES + (core + p) % CORES

    msgs = {}

    def msg(name, src, dst, peer):
        n = len(msgs)
        assert n < N_MSG
        msgs[name] = pltpu.make_async_remote_copy(
            src_ref=src, dst_ref=dst, send_sem=send_sem.at[n], recv_sem=recv_sem.at[n], device_id=peer, device_id_type=MESH)

    d_ff2, d_model2 = wd.shape[1] // 2, wg.shape[1] // 2
    wins, whs, halves = (wg_hbm, wu_hbm, wd_hbm), (whg, whu, whd), (d_model2, d_model2, d_ff2)
    for d in range(2):
        at, frm = (3, 1)[d], (3, 1)[d]
        msg(('x1', d), xyc.at[0, :, 0], xyo.at[at - 1, 0, :, 0], xpeer[d])
        msg(('x1g', d), gtc.at[0, 0], gto.at[at - 1, 0, 0], xpeer[d])
        k = 1 - d
        msg(('x2', d), xyo.at[frm - 1, 0, k, 0], xyo.at[1, 0, k, 0], xpeer[d])
        for m in range(3):
            msg(('w1', m, d), wins[m], whs[m].at[0, at], xpeer[d])
            rows = pl.ds(d * halves[m], halves[m])
            msg(('w2', m, d), whs[m].at[0, frm, rows], whs[m].at[0, 2, rows], xpeer[d])
        msg(('y1', d), xyc.at[0], xyc.at[at], ypeer[d])
        msg(('y1g', d), gtc.at[0], gtc.at[at], ypeer[d])
        msg(('y2', d), xyc.at[frm, :, d], xyc.at[2, :, d], ypeer[d])
        msg(('y2g', d), gtc.at[frm, d], gtc.at[2, d], ypeer[d])
        for i in range(3):
            msg(('y3', i, d), xyo.at[i, 0, :, 0], xyo.at[i, 0, :, at], ypeer[d])
            msg(('y3g', i, d), gto.at[i, 0, 0], gto.at[i, 0, at], ypeer[d])
            msg(('y4', i, d), xyo.at[i, 0, k, frm], xyo.at[i, 0, k, 2], ypeer[d])
        for r in range(SIDE):
            msg(('x3', r, d), xyc.at[r, :, 1], xyo.at[at - 1, 1, :, r], xpeer[d])
        msg(('x3g', d), gtc.at[:, 1], gto.at[at - 1, 1], xpeer[d])
        msg(('x4', d), xyo.at[frm - 1, 1, k], xyo.at[1, 1, k], xpeer[d])
        msg(('r1', d), con.at[2, :, d], rsh.at[d], ypeer[d])
        msg(('r1g', d), cong.at[2, d], rshg.at[d], ypeer[d])
        for h in range(2):
            src = (1, 3)[d]
            msg(('r2', h, d), con.at[src, :, h], rsf.at[d, :, h], ypeer[d])
            msg(('r2g', h, d), cong.at[src, h], rsfg.at[d, h], ypeer[d])
    msg('x2g', gto.at[0, 0, 0], gto.at[1, 0, 0], xpeer[1])
    for i in range(3):
        msg(('y4g', i), gto.at[i, 0, 1], gto.at[i, 0, 2], ypeer[1])
    msg('x4g', gto.at[0, 1], gto.at[1, 1], xpeer[1])
    for m in range(3):
        msg(('m', 0, m), wins[m], (wg, wu, wd)[m].at[1], mate)
        for i in range(1, SIDE):
            msg(('m', i, m), whs[m].at[0, i], whs[m].at[1, i], mate)
        msg(('dw', m), (dwg, dwu, dwd)[m].at[1], (dwg_out, dwu_out, dwd_out)[m].at[1], mate)

    def start(*names):
        for name in names:
            msgs[name].start()

    def arrive(*names):
        for name in names:
            msgs[name].wait_recv()

    both = range(2)
    loads = [pltpu.make_async_copy(s, t, loc_sem.at[i]) for i, (s, t) in enumerate((
        (x_hbm, xyc.at[0, 0]), (dy_hbm, xyc.at[0, 1]), (gt_hbm, gtc.at[0]),
        (wg_hbm, wg.at[0]), (wu_hbm, wu.at[0]), (wd_hbm, wd.at[0])))]
    for load in loads:
        load.start()

    barrier = pltpu.get_barrier_semaphore()
    for peer in xpeer + ypeer + (mate,):
        pl.semaphore_signal(barrier, inc=1, device_id=peer, device_id_type=MESH)
    pl.semaphore_wait(barrier, 5)

    for load in loads[:3]:
        load.wait()
    start(*[(n, d) for d in both for n in ('x1', 'x1g', 'y1', 'y1g')])
    start(*[('w1', 0, d) for d in both])
    start(*[('m', 0, m) for m in range(3)])
    for ref in (dwg, dwu, dwd):
        ref[...] = jnp.zeros_like(ref)
    for load in loads[3:]:
        load.wait()

    th, d_model = xyc.shape[3], xyc.shape[4]
    tok = 2 * th
    pk = gtc.shape[2]
    groups = th // pk
    lane = lax.broadcasted_iota(jnp.int32, (pk, LANES), 1)

    def gate_column(tables, eid):
        return jnp.concatenate([
            jnp.sum(jnp.where(lane == q * experts + eid, t, 0.0), axis=1, keepdims=True)
            for t in tables for q in range(groups)], axis=0)

    def gate_pack(column, h, eid):
        base = h * groups
        return functools.reduce(lambda p, v: p + v, [
            jnp.where(lane == q * experts + eid, column[(base + q) * pk:(base + q + 1) * pk], 0.0) for q in range(groups)])

    def acts(x, gate, w):
        xm = x * jnp.where(gate > 0.0, 1.0, 0.0).astype(BF16)
        a = dot(xm, wg[w], 1, 0)
        b = dot(xm, wu[w], 1, 0)
        sig = jax.nn.sigmoid(a)
        silu = a * sig
        return a, b, sig, silu, (silu * b).astype(BF16)

    def act_grads(g, a, b, sig, silu, w):
        dh = dot(g, wd[w], 1, 1)
        return (dh * b * sig * (1.0 + a * (1.0 - sig))).astype(BF16), (dh * silu).astype(BF16)

    def weight_grads(x, h, g, da, db, e):
        dwd[e] += dot(h, g, 0, 0)
        dwg[e] += dot(x, da, 0, 0)
        dwu[e] += dot(x, db, 0, 0)

    def column_task(r, w, eid, first, grads):
        gate = gate_column([gtc[r, 0], gtc[r, 1]], eid)
        x = xyc[r, 0].reshape(tok, d_model)
        dy32 = xyc[r, 1].reshape(tok, d_model).astype(F32)
        a, b, sig, silu, h = acts(x, gate, w)
        o = dot(h, wd[w], 1, 0).astype(BF16).astype(F32)
        yc = (gate * o).reshape(2, th, d_model)
        dg = jnp.sum(dy32 * o, axis=1, keepdims=True)
        g = (gate * dy32).astype(BF16)
        da, db = act_grads(g, a, b, sig, silu, w)
        dxc = (dot(da, wg[w], 1, 1) + dot(db, wu[w], 1, 1)).astype(BF16).astype(F32).reshape(2, th, d_model)

        if first is not None:
            @pl.when(first)
            def _():
                con[r] = jnp.zeros_like(con[r])
                cong[r] = jnp.zeros_like(cong[r])
        con[r, 0] += yc
        con[r, 1] += dxc
        for h2 in range(2):
            cong[r, h2] += gate_pack(dg, h2, eid)
        if grads is not None:
            weight_grads(x, h, g, da, db, grads)

    def other_task(i, half, pair, e):
        eid = expert_id(e, 0)
        r = 2 * pair
        gate = gate_column([gto[i, half, r], gto[i, half, r + 1]], eid)
        x = xyo[i, half, 0, pl.ds(r, 2)].reshape(tok, d_model)
        dy32 = xyo[i, half, 1, pl.ds(r, 2)].reshape(tok, d_model).astype(F32)
        a, b, sig, silu, h = acts(x, gate, e)
        g = (gate * dy32).astype(BF16)
        da, db = act_grads(g, a, b, sig, silu, e)
        weight_grads(x, h, g, da, db, e)

    def at_step(t, n):
        return pl.when(t == n)

    def own_step(t, _):
        u, e = t // 2, t % 2
        r = u + u // 2 - 2 * (u // 3)

        @at_step(t, 1)
        def _():
            arrive(*[('m', 0, m) for m in range(3)])

        @at_step(t, 2)
        def _():
            arrive(*[(n, d) for d in both for n in ('x1', 'x1g')])
            start(('x2', 0), ('x2', 1), 'x2g')
            start(*[('w1', m, d) for m in (1, 2) for d in both])
            arrive(*[(n, d) for d in both for n in ('y1', 'y1g')])
            start(*[(n, d) for d in both for n in ('y2', 'y2g')])
            start(*[(n, i, d) for i in (0, 2) for d in both for n in ('y3', 'y3g')])

        @at_step(t, 6)
        def _():
            arrive(*[(n, d) for d in both for n in ('y2', 'y2g')])
            arrive(('x2', 0), ('x2', 1), 'x2g')
            start(*[(n, 1, d) for d in both for n in ('y3', 'y3g')])

        column_task(r, e, expert_id(e, 0), e == 0, e)
        return 0

    lax.fori_loop(0, 2 * SIDE, own_step, 0)

    def early_step(t, _):
        pair, i, e = t // 6, (t % 6) // 2, t % 2
        i = 2 * i - 3 * (i // 2)

        @at_step(t, 0)
        def _():
            arrive(*[(n, j, d) for j in (0, 2) for d in both for n in ('y3', 'y3g')])
            start(*[('y4', j, d) for j in (0, 2) for d in both], ('y4g', 0), ('y4g', 2))

        @at_step(t, 4)
        def _():
            arrive(*[(n, 1, d) for d in both for n in ('y3', 'y3g')])
            start(('y4', 1, 0), ('y4', 1, 1), ('y4g', 1))
            arrive(*[('w1', m, d) for m in (0, 1) for d in both])
            start(*[('w2', m, d) for m in (0, 1) for d in both])
            start(*[('m', j, m) for j in (1, 3) for m in (0, 1)])

        @at_step(t, 6)
        def _():
            arrive(('w1', 2, 0), ('w1', 2, 1))
            start(('w2', 2, 0), ('w2', 2, 1), ('m', 1, 2), ('m', 3, 2))
            start(*[('x3', r, d) for r in range(SIDE) for d in both], ('x3g', 0), ('x3g', 1))
            arrive(*[('y4', j, d) for j in (0, 2) for d in both], ('y4g', 0), ('y4g', 2))

        @at_step(t, 10)
        def _():
            arrive(('y4', 1, 0), ('y4', 1, 1), ('y4g', 1))

        other_task(i, 0, pair, e)
        return 0

    lax.fori_loop(0, 12, early_step, 0)

    def weight_load(p, i, slot):
        return [pltpu.make_async_copy(s.at[p, i], t.at[slot], wl_sem.at[slot - 2, m])
                for m, (s, t) in enumerate(((whg, wg), (whu, wu), (whd, wd)))]

    def load_start(p, i, slot):
        for c in weight_load(p, i, slot):
            c.start()

    def load_wait(p, i, slot):
        for c in weight_load(p, i, slot):
            c.wait()

    load_start(0, 1, 2)

    def near_step(t, _):
        v, r = t // SIDE, t % SIDE
        p, i = v // 2, 1 + 2 * (v % 2)
        slot = 2 + v % 2

        @pl.when(r == 0)
        def _():
            load_wait(p, i, slot)

            @at_step(v, 0)
            def _():
                load_start(0, 3, 3)

            @at_step(v, 1)
            def _():
                arrive(*[('m', 1, m) for m in range(3)])
                load_start(1, 1, 2)

            @at_step(v, 2)
            def _():
                arrive(*[('m', 3, m) for m in range(3)])
                load_start(1, 3, 3)

        column_task(r, slot, expert_id(p, i), None, None)
        return 0

    lax.fori_loop(0, 4 * SIDE, near_step, 0)

    arrive(*[('w2', m, d) for m in range(3) for d in both])
    start(*[('m', 2, m) for m in range(3)])
    load_start(0, 2, 2)
    load_wait(0, 2, 2)

    def far_step(t, _):
        u, p = t // 2, t % 2
        r = 2 - u + 3 * (u // 2) - 2 * (u // 3)

        @at_step(t, 1)
        def _():
            arrive(*[('m', 2, m) for m in range(3)])
            load_start(1, 2, 3)
            load_wait(1, 2, 3)

        @at_step(t, 2)
        def _():
            start(*[(n, d) for d in both for n in ('r1', 'r1g')])

        @at_step(t, 6)
        def _():
            start(('r2', 1, 0), ('r2g', 1, 0), ('r2', 0, 1), ('r2g', 0, 1))

        column_task(r, 2 + p, expert_id(p, 2), None, None)
        return 0

    lax.fori_loop(0, 2 * SIDE, far_step, 0)

    for d, (r, h) in enumerate(((1, 0), (3, 1))):
        arrive(('r1', d), ('r1g', d))
        con[r, :, h] += rsh[d]
        cong[r, h] += rshg[d]
    start(('r2', 0, 0), ('r2g', 0, 0), ('r2', 1, 1), ('r2g', 1, 1))

    def late_step(t, _):
        i, pair, e = t // 4, (t % 4) // 2, t % 2
        i = 2 * i - 3 * (i // 2)

        @at_step(t, 0)
        def _():
            arrive(*[('x3', r, d) for r in range(SIDE) for d in both], ('x3g', 0), ('x3g', 1))
            start(('x4', 0), ('x4', 1), 'x4g')

        @at_step(t, 8)
        def _():
            arrive(('x4', 0), ('x4', 1), 'x4g')

        other_task(i, 1, pair, e)
        return 0

    lax.fori_loop(0, 12, late_step, 0)

    start(*[('dw', m) for m in range(3)])
    stores = [pltpu.make_async_copy(s.at[0], t.at[0], loc_sem.at[i]) for i, (s, t) in enumerate(
        ((dwg, dwg_out), (dwu, dwu_out), (dwd, dwd_out)))]
    for store in stores:
        store.start()
    arrive(*[(n, h, d) for h in range(2) for d in both for n in ('r2', 'r2g')])
    for h in range(2):
        rows = pl.ds(h * th, th)
        y_out[rows, :] = (con[0, 0, h] + rsf[0, 0, h] + rsf[1, 0, h]).astype(BF16)
        dx_out[rows, :] = (con[0, 1, h] + rsf[0, 1, h] + rsf[1, 1, h]).astype(BF16)
        dgt_out[h] = cong[0, h] + rsfg[0, h] + rsfg[1, h]
    arrive(*[('dw', m) for m in range(3)])
    for c in msgs.values():
        c.wait_send()
    for store in stores:
        store.wait()


def solution(mesh):
    experts = SIDE * SIDE * CORES
    assert mesh.shape['ei'] == SIDE and mesh.shape['eo'] == SIDE * CORES
    groups = LANES // experts
    tok_spec = P(('dp', 'ei', 'eo'), None)
    weight_spec = P(('ei', 'eo'), None, None)
    grad_spec = P(('dp', 'ei', 'eo'), None, None)
    hbm = pl.BlockSpec(memory_space=pl.ANY)
    vmem = pl.BlockSpec(memory_space=pltpu.VMEM)

    def device_layer(x_loc, idx_loc, gate_loc, wg_loc, wu_loc, wd_loc, dy_loc):
        tok, _ = idx_loc.shape
        d_model = x_loc.shape[1]
        d_ff = wg_loc.shape[2]
        th = tok // 2
        pk = th // groups
        hit = idx_loc[:, :, None] == jnp.arange(experts, dtype=jnp.int32)
        gates = jnp.sum(jnp.where(hit, gate_loc[:, :, None], 0.0), axis=1)
        gates = gates.reshape(2, groups, pk, experts).transpose(0, 2, 1, 3).reshape(2, pk, LANES)
        dma = pltpu.SemaphoreType.DMA
        shape = jax.ShapeDtypeStruct
        units = (8 * SIDE * SIDE + 16 * SIDE) * 3
        outs = pl.pallas_call(
            kernel,
            out_shape=(
                shape((tok, d_model), BF16), shape((tok, d_model), BF16), shape((2, pk, LANES), F32),
                shape((2, d_model, d_ff), F32), shape((2, d_model, d_ff), F32), shape((2, d_ff, d_model), F32),
                shape((2, SIDE, d_model, d_ff), BF16), shape((2, SIDE, d_model, d_ff), BF16), shape((2, SIDE, d_ff, d_model), BF16)),
            in_specs=[hbm] * 6,
            out_specs=(vmem,) * 3 + (hbm,) * 6,
            scratch_shapes=[
                pltpu.VMEM((SIDE, 2, 2, th, d_model), BF16),
                pltpu.VMEM((SIDE - 1, 2, 2, SIDE, th, d_model), BF16),
                pltpu.VMEM((SIDE, 2, pk, LANES), F32),
                pltpu.VMEM((SIDE - 1, 2, SIDE, pk, LANES), F32),
                pltpu.VMEM((SIDE, 2, 2, th, d_model), F32),
                pltpu.VMEM((SIDE, 2, pk, LANES), F32),
                pltpu.VMEM((2, 2, th, d_model), F32),
                pltpu.VMEM((2, pk, LANES), F32),
                pltpu.VMEM((2, 2, 2, th, d_model), F32),
                pltpu.VMEM((2, 2, pk, LANES), F32),
                pltpu.VMEM((4, d_model, d_ff), BF16), pltpu.VMEM((4, d_model, d_ff), BF16), pltpu.VMEM((4, d_ff, d_model), BF16),
                pltpu.VMEM((2, d_model, d_ff), F32), pltpu.VMEM((2, d_model, d_ff), F32), pltpu.VMEM((2, d_ff, d_model), F32),
                dma((N_MSG,)), dma((N_MSG,)), dma((6,)), dma((2, 3)),
            ],
            compiler_params=pltpu.CompilerParams(collective_id=0, has_side_effects=True, vmem_limit_bytes=67000000),
            cost_estimate=pl.CostEstimate(flops=2 * units * tok * d_model * d_ff, bytes_accessed=64 * tok * d_model, transcendentals=0),
        )(x_loc.reshape(2, th, d_model), dy_loc.reshape(2, th, d_model), gates, wg_loc[0], wu_loc[0], wd_loc[0])
        y_loc, dx_loc, dgt, dwg, dwu, dwd = outs[:6]
        dgt = dgt.reshape(2, pk, groups, experts).transpose(0, 2, 1, 3).reshape(tok, experts)
        dgate_loc = jnp.sum(jnp.where(hit, dgt[:, None, :], 0.0), axis=2)
        return y_loc, dx_loc, dgate_loc, (dwg[0] + dwg[1])[None], (dwu[0] + dwu[1])[None], (dwd[0] + dwd[1])[None]

    return jax.shard_map(device_layer, mesh=mesh, in_specs=(tok_spec, tok_spec, tok_spec, weight_spec, weight_spec, weight_spec, tok_spec), out_specs=(tok_spec, tok_spec, tok_spec, grad_spec, grad_spec, grad_spec), check_vma=False)
```

time: 553 us -> 245 us (0.44)
  waiting for transfers between devices: 300 us -> 0 us
  Pallas kernels: 0 us -> 229 us
  matrix products: 184 us -> 0 us
  blocking collectives: 21.5 us -> 0 us
  between operations: 14.3 us -> 0.68 us
  other arithmetic: 22.8 us -> 11 us
    pallas_call x0 -> x1, Pallas kernels: none -> 229 us  [device_layer(): pl.pallas_call(kernel, out_shape=(shape((tok, d_model), BF16), shape((tok...]
    reduce_scatter x2 -> x0, waiting for transfers between devices: 189 us -> none  [the longest x1 158 us: device_layer(): lax.psum_scatter(dx_rows.astype(jnp.float32), GROUP, scatter_dimension=0,...]
    dot_general x9 -> x0, matrix products: 184 us -> none  [dot(): lax.dot_general(a, b, (dims, ((), ())), preferred_element_type=jnp.float32)]
    all_gather x2 -> x0, waiting for transfers between devices: 110 us -> none  [the longest x1 71.4 us: device_layer(): x_all = lax.all_gather(x_loc, GROUP, axis=0, tiled=True)]
    all_to_all x2 -> x0, blocking collectives: 21.5 us -> none  [the longest x1 11.9 us: device_layer(): lax.all_to_all(dg.reshape(group_devs, tok_count), GROUP, 0, 0, tiled=True)]
    mul x1 -> x0, other arithmetic: 18.8 us -> none  [device_layer(): y_part = gates * o]
    add x0 -> x2, other arithmetic: none -> 9.58 us  [the longest x1 5.33 us: device_layer(): dwu[0] + dwu[1]]
  transfers between devices with their start and end apart: 4 -> 0, of which waited for: 4 -> 0; matrix products, arithmetic and copies ran while one was open for 30% -> 0% of each run, Pallas kernels for 0% -> 0%
where the time goes in v3:
time: 245 us
  Pallas kernels  229 us (93%)
  other arithmetic  11 us (4%)
  local copies, waits for them, and re-layouts  3.69 us (2%)
    pallas_call x1, Pallas kernels, device_layer(): pl.pallas_call(kernel, out_shape=(shape((tok, d_model), BF16), shape((tok...  229 us
    add x1, other arithmetic, device_layer(): dwu[0] + dwu[1]  5.33 us

profile of v3, /device:TPU:97, one launch (start us, length us, event | category | flops | bytes accessed | tf_op | source)
XLA Modules:
  0.0 244.8 jit_solution(999740260905110196)
XLA Ops:
  0.6 0.8 select_reduce_fusion.1
  1.4 0.1 reshape.32
  1.5 0.1 copy.20
  1.6 0.7 reshape.33.gt_hbm
  2.4 0.0 copy-start.3
  2.4 229.5 %shard_map.118 = (bf16[256,1024]{1,0:T(8,128)(2,1)}, bf16[256,1024]{1,0:T(8,128)(2,1)}, f32[2,32,128]{2,1,0:T(8,128)}, f32[2,1024,512]{2,1,0:T(8,128)}, f32[2,10...) custom-call(bf16[2,128,1024]{2,1,0:T(8,128)(2,1)} %bitcast.16, ...), custom_call_target="tpu_custom_call" | custom-call | flops 154618822656 | bytes 16777216 | tf_op jit(solution)/shard_map/pallas_call | solution.py:387
  231.8 0.9 reshape.34
  232.7 0.1 copy.21
  232.9 0.1 broadcast_in_dim.32
  233.0 0.0 copy-done.3
  233.0 0.6 select_reduce_fusion
  233.6 0.0 copy-start
  233.6 4.2 %slice_add_fusion = f32[1,512,1024]{2,1,0:T(8,128)} fusion(f32[2,512,1024]{2,1,0:T(8,128)} %get-tuple-element.17), kind=kLoop, calls=%fused_computation | loop fusion | flops 524288 | bytes 6291456 | tf_op jit(solution)/shard_map/add | solution.py:416
  237.9 0.0 copy-done
  237.9 0.0 copy-start.2
  237.9 0.0 copy-start.1
  237.9 5.3 %slice_add_fusion.1 = (f32[1,1024,512]{2,1,0:T(8,128)}, f32[1,1024,512]{2,1,0:T(8,128)}) fusion(f32[2,1024,512]{2,1,0:T(8,128)} %get-tuple-element.16, f32[2,1024,512]{2,1,0:T(8,128)S(1)} %copy-done), kind=kLoop, calls=%fused_computation.1 | loop fusion | flops 1048576 | bytes 12582912 | tf_op jit(solution)/shard_map/add | solution.py:416
  243.2 0.0 copy-done.2
  243.2 0.8 copy.24
  244.0 0.0 copy-done.1
  244.0 0.8 copy.25
Async XLA Ops:
  2.4 230.6 %copy-start.3 = (s32[256,8]{0,1:T(8,128)S(1)}, s32[256,8]{0,1:T(8,128)}, u32[]{:S(2)}) copy-start(s32[256,8]{0,1:T(8,128)} %param.8) | copy-start | bytes 24580
  233.6 4.3 %copy-start = (f32[2,1024,512]{2,1,0:T(8,128)S(1)}, f32[2,1024,512]{2,1,0:T(8,128)}, u32[]{:S(2)}) copy-start(f32[2,1024,512]{2,1,0:T(8,128)} %get-tuple-element.15) | copy-start | bytes 12582916
  237.9 5.3 %copy-start.2 = (bf16[256,1024]{1,0:T(8,128)(2,1)S(1)}, bf16[256,1024]{1,0:T(8,128)(2,1)}, u32[]{:S(2)}) copy-start(bf16[256,1024]{1,0:T(8,128)(2,1)} %get-tuple-element.26) | copy-start | bytes 1572868
  237.9 6.1 %copy-start.1 = (bf16[256,1024]{1,0:T(8,128)(2,1)S(1)}, bf16[256,1024]{1,0:T(8,128)(2,1)}, u32[]{:S(2)}) copy-start(bf16[256,1024]{1,0:T(8,128)(2,1)} %get-tuple-element.27) | copy-start | bytes 1572868

commit v4 on v3

--- a/solution.py
+++ b/solution.py
@@ -71,7 +71,9 @@
         for r in range(SIDE):
             msg(('x3', r, d), xyc.at[r, :, 1], xyo.at[at - 1, 1, :, r], xpeer[d])
         msg(('x3g', d), gtc.at[:, 1], gto.at[at - 1, 1], xpeer[d])
-        msg(('x4', d), xyo.at[frm - 1, 1, k], xyo.at[1, 1, k], xpeer[d])
+        for p in range(2):
+            rr = pl.ds(2 * p, 2)
+            msg(('x4', p, d), xyo.at[frm - 1, 1, k, rr], xyo.at[1, 1, k, rr], xpeer[d])
         msg(('r1', d), con.at[2, :, d], rsh.at[d], ypeer[d])
         msg(('r1g', d), cong.at[2, d], rshg.at[d], ypeer[d])
         for h in range(2):
@@ -93,8 +95,10 @@
             msgs[name].start()
 
     def arrive(*names):
-        for name in names:
-            msgs[name].wait_recv()
+        first = names[0] if isinstance(names[0], tuple) else (names[0],)
+        with jax.named_scope('wait_' + '_'.join(str(v) for v in first)):
+            for name in names:
+                msgs[name].wait_recv()
 
     both = range(2)
     loads = [pltpu.make_async_copy(s, t, loc_sem.at[i]) for i, (s, t) in enumerate((
@@ -106,10 +110,12 @@
     barrier = pltpu.get_barrier_semaphore()
     for peer in xpeer + ypeer + (mate,):
         pl.semaphore_signal(barrier, inc=1, device_id=peer, device_id_type=MESH)
-    pl.semaphore_wait(barrier, 5)
-
-    for load in loads[:3]:
-        load.wait()
+    with jax.named_scope('wait_barrier'):
+        pl.semaphore_wait(barrier, 5)
+
+    with jax.named_scope('wait_tok'):
+        for load in loads[:3]:
+            load.wait()
     start(*[(n, d) for d in both for n in ('x1', 'x1g', 'y1', 'y1g')])
     start(*[('w1', 0, d) for d in both])
     start(*[('m', 0, m) for m in range(3)])
@@ -212,14 +218,31 @@
             arrive(('x2', 0), ('x2', 1), 'x2g')
             start(*[(n, 1, d) for d in both for n in ('y3', 'y3g')])
 
-        column_task(r, e, expert_id(e, 0), e == 0, e)
-        return 0
-
-    lax.fori_loop(0, 2 * SIDE, own_step, 0)
+        with jax.named_scope('task9'):
+            column_task(r, e, expert_id(e, 0), e == 0, e)
+        return 0
+
+    with jax.named_scope('loop_own'):
+        lax.fori_loop(0, 2 * SIDE, own_step, 0)
+
+    def side_of(n):
+        return 2 * n - 3 * (n // 2)
+
+    def weight_load(p, i, slot, m):
+        s, t = ((whg, wg), (whu, wu), (whd, wd))[m]
+        return pltpu.make_async_copy(s.at[p, i], t.at[slot], wl_sem.at[slot - 2, m])
+
+    def load_start(p, i, slot, ms=(0, 1, 2)):
+        for m in ms:
+            weight_load(p, i, slot, m).start()
+
+    def load_wait(p, i, slot):
+        with jax.named_scope('wait_load'):
+            for m in range(3):
+                weight_load(p, i, slot, m).wait()
 
     def early_step(t, _):
-        pair, i, e = t // 6, (t % 6) // 2, t % 2
-        i = 2 * i - 3 * (i // 2)
+        i, e = side_of(t // 2), t % 2
 
         @at_step(t, 0)
         def _():
@@ -233,36 +256,21 @@
             arrive(*[('w1', m, d) for m in (0, 1) for d in both])
             start(*[('w2', m, d) for m in (0, 1) for d in both])
             start(*[('m', j, m) for j in (1, 3) for m in (0, 1)])
-
-        @at_step(t, 6)
-        def _():
-            arrive(('w1', 2, 0), ('w1', 2, 1))
-            start(('w2', 2, 0), ('w2', 2, 1), ('m', 1, 2), ('m', 3, 2))
-            start(*[('x3', r, d) for r in range(SIDE) for d in both], ('x3g', 0), ('x3g', 1))
-            arrive(*[('y4', j, d) for j in (0, 2) for d in both], ('y4g', 0), ('y4g', 2))
-
-        @at_step(t, 10)
-        def _():
-            arrive(('y4', 1, 0), ('y4', 1, 1), ('y4g', 1))
-
-        other_task(i, 0, pair, e)
-        return 0
-
-    lax.fori_loop(0, 12, early_step, 0)
-
-    def weight_load(p, i, slot):
-        return [pltpu.make_async_copy(s.at[p, i], t.at[slot], wl_sem.at[slot - 2, m])
-                for m, (s, t) in enumerate(((whg, wg), (whu, wu), (whd, wd)))]
-
-    def load_start(p, i, slot):
-        for c in weight_load(p, i, slot):
-            c.start()
-
-    def load_wait(p, i, slot):
-        for c in weight_load(p, i, slot):
-            c.wait()
-
-    load_start(0, 1, 2)
+            load_start(0, 1, 2, (0, 1))
+            load_start(0, 3, 3, (0, 1))
+
+        with jax.named_scope('task6o'):
+            other_task(i, 0, 0, e)
+        return 0
+
+    with jax.named_scope('loop_early'):
+        lax.fori_loop(0, 6, early_step, 0)
+
+    arrive(('w1', 2, 0), ('w1', 2, 1))
+    start(('w2', 2, 0), ('w2', 2, 1), ('m', 1, 2), ('m', 3, 2))
+    load_start(0, 1, 2, (2,))
+    load_start(0, 3, 3, (2,))
+    start(*[('x3', r, d) for r in range(SIDE) for d in both], ('x3g', 0), ('x3g', 1))
 
     def near_step(t, _):
         v, r = t // SIDE, t % SIDE
@@ -273,10 +281,6 @@
         def _():
             load_wait(p, i, slot)
 
-            @at_step(v, 0)
-            def _():
-                load_start(0, 3, 3)
-
             @at_step(v, 1)
             def _():
                 arrive(*[('m', 1, m) for m in range(3)])
@@ -287,14 +291,24 @@
                 arrive(*[('m', 3, m) for m in range(3)])
                 load_start(1, 3, 3)
 
-        column_task(r, slot, expert_id(p, i), None, None)
-        return 0
-
-    lax.fori_loop(0, 4 * SIDE, near_step, 0)
-
-    arrive(*[('w2', m, d) for m in range(3) for d in both])
-    start(*[('m', 2, m) for m in range(3)])
-    load_start(0, 2, 2)
+            @at_step(v, 3)
+            def _():
+                arrive(*[('w2', m, d) for m in (0, 1) for d in both])
+                start(('m', 2, 0), ('m', 2, 1))
+                load_start(0, 2, 2, (0, 1))
+
+        with jax.named_scope('task6c'):
+            column_task(r, slot, expert_id(p, i), None, None)
+        return 0
+
+    with jax.named_scope('loop_near'):
+        lax.fori_loop(0, 4 * SIDE, near_step, 0)
+
+    arrive(('w2', 2, 0), ('w2', 2, 1))
+    start(('m', 2, 2))
+    load_start(0, 2, 2, (2,))
+    arrive(('m', 2, 0), ('m', 2, 1))
+    load_start(1, 2, 3, (0, 1))
     load_wait(0, 2, 2)
 
     def far_step(t, _):
@@ -303,8 +317,8 @@
 
         @at_step(t, 1)
         def _():
-            arrive(*[('m', 2, m) for m in range(3)])
-            load_start(1, 2, 3)
+            arrive(('m', 2, 2))
+            load_start(1, 2, 3, (2,))
             load_wait(1, 2, 3)
 
         @at_step(t, 2)
@@ -315,10 +329,21 @@
         def _():
             start(('r2', 1, 0), ('r2g', 1, 0), ('r2', 0, 1), ('r2g', 0, 1))
 
-        column_task(r, 2 + p, expert_id(p, 2), None, None)
-        return 0
-
-    lax.fori_loop(0, 2 * SIDE, far_step, 0)
+        with jax.named_scope('task6c'):
+            column_task(r, 2 + p, expert_id(p, 2), None, None)
+        return 0
+
+    with jax.named_scope('loop_far'):
+        lax.fori_loop(0, 2 * SIDE, far_step, 0)
+
+    arrive(*[('y4', j, d) for j in range(3) for d in both], *[('y4g', j) for j in range(3)])
+
+    def rest_step(t, _):
+        other_task(side_of(t // 2), 0, 1, t % 2)
+        return 0
+
+    with jax.named_scope('loop_rest'):
+        lax.fori_loop(0, 6, rest_step, 0)
 
     for d, (r, h) in enumerate(((1, 0), (3, 1))):
         arrive(('r1', d), ('r1g', d))
@@ -327,24 +352,41 @@
     start(('r2', 0, 0), ('r2g', 0, 0), ('r2', 1, 1), ('r2g', 1, 1))
 
     def late_step(t, _):
-        i, pair, e = t // 4, (t % 4) // 2, t % 2
-        i = 2 * i - 3 * (i // 2)
+        u = t - 8
+        near_side = 1 - t // 8
+        pair = near_side * (t // 4) + (1 - near_side) * (u // 2)
+        i = near_side * 2 * ((t % 4) // 2) + (1 - near_side)
+        e = 1 - t % 2
 
         @at_step(t, 0)
         def _():
-            arrive(*[('x3', r, d) for r in range(SIDE) for d in both], ('x3g', 0), ('x3g', 1))
-            start(('x4', 0), ('x4', 1), 'x4g')
+            arrive(*[('x3', r, d) for r in (0, 1) for d in both], ('x3g', 0), ('x3g', 1))
+            start(('x4', 0, 0), ('x4', 0, 1), 'x4g')
+
+        @at_step(t, 4)
+        def _():
+            arrive(*[('x3', r, d) for r in (2, 3) for d in both])
+            start(('x4', 1, 0), ('x4', 1, 1))
 
         @at_step(t, 8)
         def _():
-            arrive(('x4', 0), ('x4', 1), 'x4g')
-
-        other_task(i, 1, pair, e)
-        return 0
-
-    lax.fori_loop(0, 12, late_step, 0)
-
-    start(*[('dw', m) for m in range(3)])
+            arrive(('x4', 0, 0), ('x4', 0, 1), 'x4g')
+
+        @at_step(t, 10)
+        def _():
+            arrive(('x4', 1, 0), ('x4', 1, 1))
+
+        @at_step(t, 11)
+        def _():
+            start(*[('dw', m) for m in range(3)])
+
+        with jax.named_scope('task6o'):
+            other_task(i, 1, pair, e)
+        return 0
+
+    with jax.named_scope('loop_late'):
+        lax.fori_loop(0, 12, late_step, 0)
+
     stores = [pltpu.make_async_copy(s.at[0], t.at[0], loc_sem.at[i]) for i, (s, t) in enumerate(
         ((dwg, dwg_out), (dwu, dwu_out), (dwd, dwd_out)))]
     for store in stores:
@@ -356,10 +398,19 @@
         dx_out[rows, :] = (con[0, 1, h] + rsf[0, 1, h] + rsf[1, 1, h]).astype(BF16)
         dgt_out[h] = cong[0, h] + rsfg[0, h] + rsfg[1, h]
     arrive(*[('dw', m) for m in range(3)])
-    for c in msgs.values():
-        c.wait_send()
-    for store in stores:
-        store.wait()
+    with jax.named_scope('wait_send_all'):
+        for c in msgs.values():
+            c.wait_send()
+    with jax.named_scope('wait_store'):
+        for store in stores:
+            store.wait()
+
+
+def finish(dwg_ref, dwu_ref, dwd_ref, y_ref, dx_ref, dwg_out, dwu_out, dwd_out, y_out, dx_out):
+    for src, out in ((dwg_ref, dwg_out), (dwu_ref, dwu_out), (dwd_ref, dwd_out)):
+        out[0] = src[0] + src[1]
+    y_out[...] = y_ref[...]
+    dx_out[...] = dx_ref[...]
 
 
 def solution(mesh):
@@ -411,8 +462,21 @@
             cost_estimate=pl.CostEstimate(flops=2 * units * tok * d_model * d_ff, bytes_accessed=64 * tok * d_model, transcendentals=0),
         )(x_loc.reshape(2, th, d_model), dy_loc.reshape(2, th, d_model), gates, wg_loc[0], wu_loc[0], wd_loc[0])
         y_loc, dx_loc, dgt, dwg, dwu, dwd = outs[:6]
+        cut = 8
+        pair_spec = lambda rows, cols: pl.BlockSpec((2, rows // cut, cols), lambda n: (0, n, 0))
+        one_spec = lambda rows, cols: pl.BlockSpec((1, rows // cut, cols), lambda n: (0, n, 0))
+        row_spec = pl.BlockSpec((tok // cut, d_model), lambda n: (n, 0))
+        dwg, dwu, dwd, y_loc, dx_loc = pl.pallas_call(
+            finish,
+            grid=(cut,),
+            out_shape=(shape((1, d_model, d_ff), F32), shape((1, d_model, d_ff), F32), shape((1, d_ff, d_model), F32),
+                       shape((tok, d_model), BF16), shape((tok, d_model), BF16)),
+            in_specs=[pair_spec(d_model, d_ff), pair_spec(d_model, d_ff), pair_spec(d_ff, d_model), row_spec, row_spec],
+            out_specs=(one_spec(d_model, d_ff), one_spec(d_model, d_ff), one_spec(d_ff, d_model), row_spec, row_spec),
+            cost_estimate=pl.CostEstimate(flops=3 * d_model * d_ff, bytes_accessed=36 * d_model * d_ff, transcendentals=0),
+        )(dwg, dwu, dwd, y_loc, dx_loc)
         dgt = dgt.reshape(2, pk, groups, experts).transpose(0, 2, 1, 3).reshape(tok, experts)
         dgate_loc = jnp.sum(jnp.where(hit, dgt[:, None, :], 0.0), axis=2)
-        return y_loc, dx_loc, dgate_loc, (dwg[0] + dwg[1])[None], (dwu[0] + dwu[1])[None], (dwd[0] + dwd[1])[None]
+        return y_loc, dx_loc, dgate_loc, dwg, dwu, dwd
 
     return jax.shard_map(device_layer, mesh=mesh, in_specs=(tok_spec, tok_spec, tok_spec, weight_spec, weight_spec, weight_spec, tok_spec), out_specs=(tok_spec, tok_spec, tok_spec, grad_spec, grad_spec, grad_spec), check_vma=False)

time: 245 us -> 227 us (0.927)
  other arithmetic: 11 us -> 1.39 us
  Pallas kernels: 229 us -> 223 us
    pallas_call x1, Pallas kernels: 229 us -> 213 us  [device_layer(): pl.pallas_call(kernel, out_shape=(shape((tok, d_model), BF16), shape((tok...]
    add x2 -> x0, other arithmetic: 9.58 us -> none  [the longest x1 5.33 us: device_layer(): dwu[0] + dwu[1]]
    pallas_call x0 -> x1, Pallas kernels: none -> 9.51 us  [device_layer(): pl.pallas_call(finish, grid=(cut,), out_shape=(shape((1, d_model, d_ff),...]
where the time goes in v4:
time: 227 us; the launch traced here: 226 us
  Pallas kernels  223 us (98%)
    pallas_call x1, Pallas kernels, device_layer(): pl.pallas_call(kernel, out_shape=(shape((tok, d_model), BF16), shape((tok...  213 us
    pallas_call x1, Pallas kernels, device_layer(): pl.pallas_call(finish, grid=(cut,), out_shape=(shape((1, d_model, d_ff),...  9.51 us

profile of v4, /device:TPU:97, one launch (start us, length us, event | category | flops | bytes accessed | tf_op | source)
XLA Modules:
  0.0 226.3 jit_solution(10604690544502058474)
XLA Ops:
  0.6 0.8 select_reduce_fusion.1
  1.4 0.1 reshape.32
  1.5 0.1 copy.20
  1.6 0.7 reshape.33.gt_hbm
  2.4 213.3 %shard_map.118 = (bf16[256,1024]{1,0:T(8,128)(2,1)}, bf16[256,1024]{1,0:T(8,128)(2,1)}, f32[2,32,128]{2,1,0:T(8,128)}, f32[2,1024,512]{2,1,0:T(8,128)}, f32[2,10...) custom-call(bf16[2,128,1024]{2,1,0:T(8,128)(2,1)} %bitcast.16, ...), custom_call_target="tpu_custom_call" | custom-call | flops 154618822656 | bytes 16777216 | tf_op jit(solution)/shard_map/pallas_call | solution.py:438
  215.7 0.0 copy-start
  215.7 0.0 copy-start.1
  215.7 9.5 %shard_map.119 = (f32[1,1024,512]{2,1,0:T(8,128)}, f32[1,1024,512]{2,1,0:T(8,128)}, f32[1,512,1024]{2,1,0:T(8,128)}, bf16[256,1024]{1,0:T(8,128)(2,1)}, bf16[256,1024]{1,0:T(8,128)(2,1)}) custom-call(f32[2,1024,512]{2,1,0:T(8,128)} %get-tuple-element.17.dwg_ref, f32[2,1024,512]{2,1,0:T(8,128)} %get-tuple-element.18.dwu_ref, ...), custom_call_target="tpu_custom_call" | custom-call | flops 1572864 | bytes 18874368 | tf_op jit(solution)/shard_map/pallas_call | solution.py:469
  225.2 0.0 copy-done
  225.2 0.1 reshape.34
  225.4 0.1 copy.21
  225.5 0.1 broadcast_in_dim.29
  225.6 0.0 copy-done.1
  225.6 0.6 select_reduce_fusion
Async XLA Ops:
  215.7 9.5 %copy-start = (f32[2,32,128]{2,1,0:T(8,128)S(1)}, f32[2,32,128]{2,1,0:T(8,128)}, u32[]{:S(2)}) copy-start(f32[2,32,128]{2,1,0:T(8,128)} %get-tuple-element.24) | copy-start | bytes 98308
  215.7 9.9 %copy-start.1 = (s32[256,8]{0,1:T(8,128)S(1)}, s32[256,8]{0,1:T(8,128)}, u32[]{:S(2)}) copy-start(s32[256,8]{0,1:T(8,128)} %param.8) | copy-start | bytes 24580

commit v5 on v3

--- a/solution.py
+++ b/solution.py
@@ -23,7 +23,7 @@
 def kernel(x_hbm, dy_hbm, gt_hbm, wg_hbm, wu_hbm, wd_hbm,
            y_out, dx_out, dgt_out, dwg_out, dwu_out, dwd_out, whg, whu, whd,
            xyc, xyo, gtc, gto, con, cong, rsh, rshg, rsf, rsfg, wg, wu, wd, dwg, dwu, dwd,
-           send_sem, recv_sem, loc_sem, wl_sem):
+           send_sem, recv_sem, loc_sem, wl_sem, free_sem):
     dp = lax.axis_index('dp')
     row = lax.axis_index('ei')
     eo = lax.axis_index('eo')
@@ -40,6 +40,16 @@
     def expert_id(p, i):
         return row * SIDE * CORES + ((col + i) % SIDE) * CORES + (core + p) % CORES
 
+    def loop(n, body):
+        def run(t, carry):
+            body(t)
+            return carry
+        lax.fori_loop(0, n, run, 0)
+
+    def two(*key):
+        return [key + (d,) for d in both]
+
+    both, sides, mats = range(2), (1, 3), range(3)
     msgs = {}
 
     def msg(name, src, dst, peer):
@@ -50,13 +60,13 @@
 
     d_ff2, d_model2 = wd.shape[1] // 2, wg.shape[1] // 2
     wins, whs, halves = (wg_hbm, wu_hbm, wd_hbm), (whg, whu, whd), (d_model2, d_model2, d_ff2)
-    for d in range(2):
-        at, frm = (3, 1)[d], (3, 1)[d]
+    for d in both:
+        at = frm = sides[1 - d]
         msg(('x1', d), xyc.at[0, :, 0], xyo.at[at - 1, 0, :, 0], xpeer[d])
         msg(('x1g', d), gtc.at[0, 0], gto.at[at - 1, 0, 0], xpeer[d])
         k = 1 - d
         msg(('x2', d), xyo.at[frm - 1, 0, k, 0], xyo.at[1, 0, k, 0], xpeer[d])
-        for m in range(3):
+        for m in mats:
             msg(('w1', m, d), wins[m], whs[m].at[0, at], xpeer[d])
             rows = pl.ds(d * halves[m], halves[m])
             msg(('w2', m, d), whs[m].at[0, frm, rows], whs[m].at[0, 2, rows], xpeer[d])
@@ -64,25 +74,30 @@
         msg(('y1g', d), gtc.at[0], gtc.at[at], ypeer[d])
         msg(('y2', d), xyc.at[frm, :, d], xyc.at[2, :, d], ypeer[d])
         msg(('y2g', d), gtc.at[frm, d], gtc.at[2, d], ypeer[d])
-        for i in range(3):
+        for i in mats:
             msg(('y3', i, d), xyo.at[i, 0, :, 0], xyo.at[i, 0, :, at], ypeer[d])
             msg(('y3g', i, d), gto.at[i, 0, 0], gto.at[i, 0, at], ypeer[d])
             msg(('y4', i, d), xyo.at[i, 0, k, frm], xyo.at[i, 0, k, 2], ypeer[d])
         for r in range(SIDE):
             msg(('x3', r, d), xyc.at[r, :, 1], xyo.at[at - 1, 1, :, r], xpeer[d])
         msg(('x3g', d), gtc.at[:, 1], gto.at[at - 1, 1], xpeer[d])
-        msg(('x4', d), xyo.at[frm - 1, 1, k], xyo.at[1, 1, k], xpeer[d])
+        for p in both:
+            rr = pl.ds(2 * p, 2)
+            msg(('x4', p, d), xyo.at[frm - 1, 1, k, rr], xyo.at[1, 1, k, rr], xpeer[d])
         msg(('r1', d), con.at[2, :, d], rsh.at[d], ypeer[d])
         msg(('r1g', d), cong.at[2, d], rshg.at[d], ypeer[d])
-        for h in range(2):
-            src = (1, 3)[d]
+        for h in both:
+            src = sides[d]
             msg(('r2', h, d), con.at[src, :, h], rsf.at[d, :, h], ypeer[d])
             msg(('r2g', h, d), cong.at[src, h], rsfg.at[d, h], ypeer[d])
     msg('x2g', gto.at[0, 0, 0], gto.at[1, 0, 0], xpeer[1])
-    for i in range(3):
+    for i in mats:
         msg(('y4g', i), gto.at[i, 0, 1], gto.at[i, 0, 2], ypeer[1])
     msg('x4g', gto.at[0, 1], gto.at[1, 1], xpeer[1])
-    for m in range(3):
+    rr = pl.ds(2, 2)
+    msg('tok', xyo.at[1, 1, :, rr], xyo.at[0, 0, :, rr], mate)
+    msg('tokg', gto.at[1, 1, rr], gto.at[0, 0, rr], mate)
+    for m in mats:
         msg(('m', 0, m), wins[m], (wg, wu, wd)[m].at[1], mate)
         for i in range(1, SIDE):
             msg(('m', i, m), whs[m].at[0, i], whs[m].at[1, i], mate)
@@ -96,7 +111,6 @@
         for name in names:
             msgs[name].wait_recv()
 
-    both = range(2)
     loads = [pltpu.make_async_copy(s, t, loc_sem.at[i]) for i, (s, t) in enumerate((
         (x_hbm, xyc.at[0, 0]), (dy_hbm, xyc.at[0, 1]), (gt_hbm, gtc.at[0]),
         (wg_hbm, wg.at[0]), (wu_hbm, wu.at[0]), (wd_hbm, wd.at[0])))]
@@ -111,8 +125,8 @@
     for load in loads[:3]:
         load.wait()
     start(*[(n, d) for d in both for n in ('x1', 'x1g', 'y1', 'y1g')])
-    start(*[('w1', 0, d) for d in both])
-    start(*[('m', 0, m) for m in range(3)])
+    start(*two('w1', 0))
+    start(*[('m', 0, m) for m in mats])
     for ref in (dwg, dwu, dwd):
         ref[...] = jnp.zeros_like(ref)
     for load in loads[3:]:
@@ -170,7 +184,7 @@
                 cong[r] = jnp.zeros_like(cong[r])
         con[r, 0] += yc
         con[r, 1] += dxc
-        for h2 in range(2):
+        for h2 in both:
             cong[r, h2] += gate_pack(dg, h2, eid)
         if grads is not None:
             weight_grads(x, h, g, da, db, grads)
@@ -189,18 +203,18 @@
     def at_step(t, n):
         return pl.when(t == n)
 
-    def own_step(t, _):
+    def own_step(t):
         u, e = t // 2, t % 2
         r = u + u // 2 - 2 * (u // 3)
 
         @at_step(t, 1)
         def _():
-            arrive(*[('m', 0, m) for m in range(3)])
+            arrive(*[('m', 0, m) for m in mats])
 
         @at_step(t, 2)
         def _():
             arrive(*[(n, d) for d in both for n in ('x1', 'x1g')])
-            start(('x2', 0), ('x2', 1), 'x2g')
+            start(*two('x2'), 'x2g')
             start(*[('w1', m, d) for m in (1, 2) for d in both])
             arrive(*[(n, d) for d in both for n in ('y1', 'y1g')])
             start(*[(n, d) for d in both for n in ('y2', 'y2g')])
@@ -209,17 +223,30 @@
         @at_step(t, 6)
         def _():
             arrive(*[(n, d) for d in both for n in ('y2', 'y2g')])
-            arrive(('x2', 0), ('x2', 1), 'x2g')
+            arrive(*two('x2'), 'x2g')
             start(*[(n, 1, d) for d in both for n in ('y3', 'y3g')])
 
         column_task(r, e, expert_id(e, 0), e == 0, e)
-        return 0
-
-    lax.fori_loop(0, 2 * SIDE, own_step, 0)
-
-    def early_step(t, _):
-        pair, i, e = t // 6, (t % 6) // 2, t % 2
-        i = 2 * i - 3 * (i // 2)
+
+    loop(2 * SIDE, own_step)
+
+    def side_of(n):
+        return 2 * n - 3 * (n // 2)
+
+    def weight_load(p, i, slot, m):
+        s, t = ((whg, wg), (whu, wu), (whd, wd))[m]
+        return pltpu.make_async_copy(s.at[p, i], t.at[slot], wl_sem.at[slot - 2, m])
+
+    def load_start(p, i, slot, ms=mats):
+        for m in ms:
+            weight_load(p, i, slot, m).start()
+
+    def load_wait(p, i, slot):
+        for m in mats:
+            weight_load(p, i, slot, m).wait()
+
+    def early_step(t):
+        i, e = side_of(t // 2), t % 2
 
         @at_step(t, 0)
         def _():
@@ -229,82 +256,70 @@
         @at_step(t, 4)
         def _():
             arrive(*[(n, 1, d) for d in both for n in ('y3', 'y3g')])
-            start(('y4', 1, 0), ('y4', 1, 1), ('y4g', 1))
-            arrive(*[('w1', m, d) for m in (0, 1) for d in both])
-            start(*[('w2', m, d) for m in (0, 1) for d in both])
-            start(*[('m', j, m) for j in (1, 3) for m in (0, 1)])
-
-        @at_step(t, 6)
-        def _():
-            arrive(('w1', 2, 0), ('w1', 2, 1))
-            start(('w2', 2, 0), ('w2', 2, 1), ('m', 1, 2), ('m', 3, 2))
-            start(*[('x3', r, d) for r in range(SIDE) for d in both], ('x3g', 0), ('x3g', 1))
-            arrive(*[('y4', j, d) for j in (0, 2) for d in both], ('y4g', 0), ('y4g', 2))
-
-        @at_step(t, 10)
-        def _():
-            arrive(('y4', 1, 0), ('y4', 1, 1), ('y4g', 1))
-
-        other_task(i, 0, pair, e)
-        return 0
-
-    lax.fori_loop(0, 12, early_step, 0)
-
-    def weight_load(p, i, slot):
-        return [pltpu.make_async_copy(s.at[p, i], t.at[slot], wl_sem.at[slot - 2, m])
-                for m, (s, t) in enumerate(((whg, wg), (whu, wu), (whd, wd)))]
-
-    def load_start(p, i, slot):
-        for c in weight_load(p, i, slot):
-            c.start()
-
-    def load_wait(p, i, slot):
-        for c in weight_load(p, i, slot):
-            c.wait()
-
-    load_start(0, 1, 2)
-
-    def near_step(t, _):
-        v, r = t // SIDE, t % SIDE
-        p, i = v // 2, 1 + 2 * (v % 2)
-        slot = 2 + v % 2
-
-        @pl.when(r == 0)
+            start(*two('y4', 1), ('y4g', 1))
+            arrive(*[('w1', m, d) for m in both for d in both])
+            start(*[('w2', m, d) for m in both for d in both])
+            start(*[('m', j, m) for j in sides for m in both])
+            load_start(0, 1, 2, both)
+            load_start(0, 3, 3, both)
+
+        other_task(i, 0, 0, e)
+
+    loop(6, early_step)
+
+    arrive(*two('w1', 2))
+    start(*two('w2', 2), *[('m', j, 2) for j in sides])
+    load_start(0, 1, 2, (2,))
+    load_start(0, 3, 3, (2,))
+    start(*[('x3', r, d) for r in range(SIDE) for d in both], *two('x3g'))
+
+    def near_expert(v):
+        return v // 2, 1 + 2 * (v % 2), 2 + v % 2
+
+    def near_step(t):
+        v = t // 3 - t // 12
+        r = (1 + t - 3 * v) % SIDE
+        p, i, slot = near_expert(v)
+
+        @pl.when(r == 1)
         def _():
             load_wait(p, i, slot)
-
-            @at_step(v, 0)
-            def _():
-                load_start(0, 3, 3)
 
             @at_step(v, 1)
             def _():
-                arrive(*[('m', 1, m) for m in range(3)])
+                arrive(*[('m', 1, m) for m in mats])
                 load_start(1, 1, 2)
 
             @at_step(v, 2)
             def _():
-                arrive(*[('m', 3, m) for m in range(3)])
+                arrive(*[('m', 3, m) for m in mats])
                 load_start(1, 3, 3)
 
+            @at_step(v, 3)
+            def _():
+                arrive(*[('w2', m, d) for m in both for d in both])
+                start(*two('m', 2))
+                load_start(0, 2, 2, both)
+
         column_task(r, slot, expert_id(p, i), None, None)
-        return 0
-
-    lax.fori_loop(0, 4 * SIDE, near_step, 0)
-
-    arrive(*[('w2', m, d) for m in range(3) for d in both])
-    start(*[('m', 2, m) for m in range(3)])
-    load_start(0, 2, 2)
+
+    loop(13, near_step)
+
+    arrive(*two('w2', 2))
+    start(('m', 2, 2))
+    load_start(0, 2, 2, (2,))
+    arrive(*two('m', 2))
+    load_start(1, 2, 3, both)
     load_wait(0, 2, 2)
 
-    def far_step(t, _):
+    def far_step(t):
         u, p = t // 2, t % 2
         r = 2 - u + 3 * (u // 2) - 2 * (u // 3)
 
         @at_step(t, 1)
         def _():
-            arrive(*[('m', 2, m) for m in range(3)])
-            load_start(1, 2, 3)
+            arrive(('m', 2, 2))
+            load_start(1, 2, 3, (2,))
             load_wait(1, 2, 3)
 
         @at_step(t, 2)
@@ -316,50 +331,113 @@
             start(('r2', 1, 0), ('r2g', 1, 0), ('r2', 0, 1), ('r2g', 0, 1))
 
         column_task(r, 2 + p, expert_id(p, 2), None, None)
-        return 0
-
-    lax.fori_loop(0, 2 * SIDE, far_step, 0)
-
-    for d, (r, h) in enumerate(((1, 0), (3, 1))):
+
+    loop(2 * SIDE, far_step)
+
+    load_start(0, 1, 2)
+    load_start(0, 3, 3)
+    arrive(*[('y4', j, d) for j in mats for d in both], *[('y4g', j) for j in mats])
+
+    def rest_step(t):
+        other_task(side_of(t // 2), 0, 1, t % 2)
+
+    loop(6, rest_step)
+
+    for d in both:
+        msgs.pop(('y4', 0, d)).wait_send()
+    pl.semaphore_signal(free_sem, inc=1, device_id=mate, device_id_type=MESH)
+
+    for d, (r, h) in enumerate(zip(sides, both)):
         arrive(('r1', d), ('r1g', d))
         con[r, :, h] += rsh[d]
         cong[r, h] += rshg[d]
     start(('r2', 0, 0), ('r2g', 0, 0), ('r2', 1, 1), ('r2g', 1, 1))
 
-    def late_step(t, _):
-        i, pair, e = t // 4, (t % 4) // 2, t % 2
-        i = 2 * i - 3 * (i // 2)
+    def last_step(v):
+        p, i, slot = near_expert(v)
+        load_wait(p, i, slot)
+        column_task(0, slot, expert_id(p, i), None, None)
+
+        @at_step(v, 0)
+        def _():
+            load_start(1, 1, 2)
+
+    loop(3, last_step)
+
+    def late_step(t):
+        far, tail, last = t // 8, t // 10, t // 11
+        pair = (1 - far) * (t // 4) + far * tail
+        i = (1 - far) * 2 * ((t % 4) // 2) + far * (1 - last)
+        e = (1 - t % 2) * (1 - tail)
 
         @at_step(t, 0)
         def _():
-            arrive(*[('x3', r, d) for r in range(SIDE) for d in both], ('x3g', 0), ('x3g', 1))
-            start(('x4', 0), ('x4', 1), 'x4g')
+            arrive(*[('x3', r, d) for r in (0, 1) for d in both], *two('x3g'))
+            start(*two('x4', 0), 'x4g')
+
+        @at_step(t, 4)
+        def _():
+            arrive(*[('x3', r, d) for r in (2, 3) for d in both])
+            start(*two('x4', 1))
 
         @at_step(t, 8)
         def _():
-            arrive(('x4', 0), ('x4', 1), 'x4g')
-
-        other_task(i, 1, pair, e)
-        return 0
-
-    lax.fori_loop(0, 12, late_step, 0)
-
-    start(*[('dw', m) for m in range(3)])
+            arrive(*two('x4', 0), 'x4g')
+
+        @at_step(t, 10)
+        def _():
+            arrive(*two('x4', 1))
+            pl.semaphore_wait(free_sem, 1)
+            start('tok', 'tokg')
+
+        @at_step(t, 11)
+        def _():
+            arrive('tok', 'tokg')
+
+        @at_step(t, 9)
+        def _():
+            start(*[('dw', m) for m in mats])
+
+        other_task(i, 1 - last, pair, e)
+
+    loop(12, late_step)
+
     stores = [pltpu.make_async_copy(s.at[0], t.at[0], loc_sem.at[i]) for i, (s, t) in enumerate(
         ((dwg, dwg_out), (dwu, dwu_out), (dwd, dwd_out)))]
     for store in stores:
         store.start()
-    arrive(*[(n, h, d) for h in range(2) for d in both for n in ('r2', 'r2g')])
-    for h in range(2):
+    arrive(*[(n, h, d) for h in both for d in both for n in ('r2', 'r2g')])
+    for h in both:
         rows = pl.ds(h * th, th)
         y_out[rows, :] = (con[0, 0, h] + rsf[0, 0, h] + rsf[1, 0, h]).astype(BF16)
         dx_out[rows, :] = (con[0, 1, h] + rsf[0, 1, h] + rsf[1, 1, h]).astype(BF16)
         dgt_out[h] = cong[0, h] + rsfg[0, h] + rsfg[1, h]
-    arrive(*[('dw', m) for m in range(3)])
+    arrive(*[('dw', m) for m in mats])
     for c in msgs.values():
         c.wait_send()
     for store in stores:
         store.wait()
+
+
+def finish(cut, dwg_in, dwu_in, dwd_in, y_in, dx_in, dwg_out, dwu_out, dwd_out, y_out, dx_out, bg, bu, bd, by, bx, in_sem, out_sem):
+    jobs = []
+    for m, (src, buf, out) in enumerate(((dwg_in, bg, dwg_out), (dwu_in, bu, dwu_out), (dwd_in, bd, dwd_out))):
+        rows = buf.shape[1] // cut
+        for n in range(cut):
+            part = pl.ds(n * rows, rows)
+            jobs.append((pltpu.make_async_copy(src.at[:, part], buf.at[:, part], in_sem.at[m, n]),
+                         pltpu.make_async_copy(buf.at[0, part], out.at[0, part], out_sem.at[m, n]), buf, part))
+    for m, (src, buf, out) in enumerate(((y_in, by, y_out), (dx_in, bx, dx_out))):
+        jobs.append((pltpu.make_async_copy(src, buf, in_sem.at[3, m]), pltpu.make_async_copy(buf, out, out_sem.at[3, m]), None, None))
+    for job in jobs:
+        job[0].start()
+    for read, write, buf, part in jobs:
+        read.wait()
+        if buf is not None:
+            buf[0, part, :] += buf[1, part, :]
+        write.start()
+    for job in jobs:
+        job[1].wait()
 
 
 def solution(mesh):
@@ -405,14 +483,26 @@
                 pltpu.VMEM((2, 2, pk, LANES), F32),
                 pltpu.VMEM((4, d_model, d_ff), BF16), pltpu.VMEM((4, d_model, d_ff), BF16), pltpu.VMEM((4, d_ff, d_model), BF16),
                 pltpu.VMEM((2, d_model, d_ff), F32), pltpu.VMEM((2, d_model, d_ff), F32), pltpu.VMEM((2, d_ff, d_model), F32),
-                dma((N_MSG,)), dma((N_MSG,)), dma((6,)), dma((2, 3)),
+                dma((N_MSG,)), dma((N_MSG,)), dma((6,)), dma((2, 3)), pltpu.SemaphoreType.REGULAR,
             ],
             compiler_params=pltpu.CompilerParams(collective_id=0, has_side_effects=True, vmem_limit_bytes=67000000),
             cost_estimate=pl.CostEstimate(flops=2 * units * tok * d_model * d_ff, bytes_accessed=64 * tok * d_model, transcendentals=0),
         )(x_loc.reshape(2, th, d_model), dy_loc.reshape(2, th, d_model), gates, wg_loc[0], wu_loc[0], wd_loc[0])
         y_loc, dx_loc, dgt, dwg, dwu, dwd = outs[:6]
+        cut = 4
+        wide, tall, rows = (d_model, d_ff), (d_ff, d_model), (tok, d_model)
+        dwg, dwu, dwd, y_loc, dx_loc = pl.pallas_call(
+            functools.partial(finish, cut),
+            out_shape=(shape((1,) + wide, F32), shape((1,) + wide, F32), shape((1,) + tall, F32), shape(rows, BF16), shape(rows, BF16)),
+            in_specs=[hbm] * 5,
+            out_specs=(hbm,) * 5,
+            scratch_shapes=[pltpu.VMEM((2,) + wide, F32), pltpu.VMEM((2,) + wide, F32), pltpu.VMEM((2,) + tall, F32),
+                            pltpu.VMEM(rows, BF16), pltpu.VMEM(rows, BF16), dma((4, cut)), dma((4, cut))],
+            compiler_params=pltpu.CompilerParams(vmem_limit_bytes=60000000),
+            cost_estimate=pl.CostEstimate(flops=3 * d_model * d_ff, bytes_accessed=36 * d_model * d_ff, transcendentals=0),
+        )(dwg, dwu, dwd, y_loc, dx_loc)
         dgt = dgt.reshape(2, pk, groups, experts).transpose(0, 2, 1, 3).reshape(tok, experts)
         dgate_loc = jnp.sum(jnp.where(hit, dgt[:, None, :], 0.0), axis=2)
-        return y_loc, dx_loc, dgate_loc, (dwg[0] + dwg[1])[None], (dwu[0] + dwu[1])[None], (dwd[0] + dwd[1])[None]
+        return y_loc, dx_loc, dgate_loc, dwg, dwu, dwd
 
     return jax.shard_map(device_layer, mesh=mesh, in_specs=(tok_spec, tok_spec, tok_spec, weight_spec, weight_spec, weight_spec, tok_spec), out_specs=(tok_spec, tok_spec, tok_spec, grad_spec, grad_spec, grad_spec), check_vma=False)

time: 245 us -> 224 us (0.914)
  other arithmetic: 11 us -> 1.39 us
  Pallas kernels: 229 us -> 220 us
    pallas_call x1, Pallas kernels: 229 us -> 212 us  [device_layer(): pl.pallas_call(kernel, out_shape=(shape((tok, d_model), BF16), shape((tok...]
    add x2 -> x0, other arithmetic: 9.58 us -> none  [the longest x1 5.33 us: device_layer(): dwu[0] + dwu[1]]
    pallas_call x0 -> x1, Pallas kernels: none -> 7.81 us  [device_layer(): pl.pallas_call(functools.partial(finish, cut), out_shape=(shape((1,) + wi...]
where the time goes in v5:
time: 224 us
  Pallas kernels  220 us (98%)
    pallas_call x1, Pallas kernels, device_layer(): pl.pallas_call(kernel, out_shape=(shape((tok, d_model), BF16), shape((tok...  212 us
    pallas_call x1, Pallas kernels, device_layer(): pl.pallas_call(functools.partial(finish, cut), out_shape=(shape((1,) + wi...  7.81 us

profile of v5, /device:TPU:97, one launch (start us, length us, event | category | flops | bytes accessed | tf_op | source)
XLA Modules:
  0.0 223.7 jit_solution(15665906149292241712)
XLA Ops:
  0.6 0.8 select_reduce_fusion.1
  1.4 0.1 reshape.32
  1.5 0.1 copy.20
  1.6 0.7 reshape.33.gt_hbm
  2.4 212.5 %shard_map.118 = (bf16[256,1024]{1,0:T(8,128)(2,1)}, bf16[256,1024]{1,0:T(8,128)(2,1)}, f32[2,32,128]{2,1,0:T(8,128)}, f32[2,1024,512]{2,1,0:T(8,128)}, f32[2,10...) custom-call(bf16[2,128,1024]{2,1,0:T(8,128)(2,1)} %bitcast.16, ...), custom_call_target="tpu_custom_call" | custom-call | flops 154618822656 | bytes 16777216 | tf_op jit(solution)/shard_map/pallas_call | solution.py:465
  214.8 0.0 copy-start
  214.8 0.0 copy-start.1
  214.9 7.8 %shard_map.119 = (f32[1,1024,512]{2,1,0:T(8,128)}, f32[1,1024,512]{2,1,0:T(8,128)}, f32[1,512,1024]{2,1,0:T(8,128)}, bf16[256,1024]{1,0:T(8,128)(2,1)}, bf16[256,1024]{1,0:T(8,128)(2,1)}) custom-call(f32[2,1024,512]{2,1,0:T(8,128)} %get-tuple-element.17.dwg_in, f32[2,1024,512]{2,1,0:T(8,128)} %get-tuple-element.18.dwu_in, ...), custom_call_target="tpu_custom_call" | custom-call | flops 1572864 | bytes 18874368 | tf_op jit(solution)/shard_map/pallas_call | solution.py:494
  222.7 0.0 copy-done
  222.7 0.1 reshape.34
  222.8 0.1 copy.21
  222.9 0.1 broadcast_in_dim.29
  223.1 0.0 copy-done.1
  223.1 0.6 select_reduce_fusion
Async XLA Ops:
  214.8 7.8 %copy-start = (f32[2,32,128]{2,1,0:T(8,128)S(1)}, f32[2,32,128]{2,1,0:T(8,128)}, u32[]{:S(2)}) copy-start(f32[2,32,128]{2,1,0:T(8,128)} %get-tuple-element.24) | copy-start | bytes 98308
  214.8 8.2 %copy-start.1 = (s32[256,8]{0,1:T(8,128)S(1)}, s32[256,8]{0,1:T(8,128)}, u32[]{:S(2)}) copy-start(s32[256,8]{0,1:T(8,128)} %param.8) | copy-start | bytes 24580

commit v6 on v5

--- a/solution.py
+++ b/solution.py
@@ -11,6 +11,7 @@
 SIDE = 4
 CORES = 2
 LANES = 128
+FAR = 4
 F32 = jnp.float32
 BF16 = jnp.bfloat16
 N_MSG = 96
@@ -23,7 +24,7 @@
 def kernel(x_hbm, dy_hbm, gt_hbm, wg_hbm, wu_hbm, wd_hbm,
            y_out, dx_out, dgt_out, dwg_out, dwu_out, dwd_out, whg, whu, whd,
            xyc, xyo, gtc, gto, con, cong, rsh, rshg, rsf, rsfg, wg, wu, wd, dwg, dwu, dwd,
-           send_sem, recv_sem, loc_sem, wl_sem, free_sem):
+           send_sem, recv_sem, loc_sem, wl_sem, free_sem, slot_sem):
     dp = lax.axis_index('dp')
     row = lax.axis_index('ei')
     eo = lax.axis_index('eo')
@@ -69,7 +70,8 @@
         for m in mats:
             msg(('w1', m, d), wins[m], whs[m].at[0, at], xpeer[d])
             rows = pl.ds(d * halves[m], halves[m])
-            msg(('w2', m, d), whs[m].at[0, frm, rows], whs[m].at[0, 2, rows], xpeer[d])
+            far_dst = wd.at[FAR, rows] if m == 2 else whs[m].at[0, 2, rows]
+            msg(('w2', m, d), whs[m].at[0, frm, rows], far_dst, xpeer[d])
         msg(('y1', d), xyc.at[0], xyc.at[at], ypeer[d])
         msg(('y1g', d), gtc.at[0], gtc.at[at], ypeer[d])
         msg(('y2', d), xyc.at[frm, :, d], xyc.at[2, :, d], ypeer[d])
@@ -100,7 +102,8 @@
     for m in mats:
         msg(('m', 0, m), wins[m], (wg, wu, wd)[m].at[1], mate)
         for i in range(1, SIDE):
-            msg(('m', i, m), whs[m].at[0, i], whs[m].at[1, i], mate)
+            near = i != 2 or m != 2
+            msg(('m', i, m), whs[m].at[0, i] if near else wd.at[FAR], whs[m].at[1, i] if near else wd.at[2], mate)
         msg(('dw', m), (dwg, dwu, dwd)[m].at[1], (dwg_out, dwu_out, dwd_out)[m].at[1], mate)
 
     def start(*names):
@@ -156,8 +159,8 @@
         silu = a * sig
         return a, b, sig, silu, (silu * b).astype(BF16)
 
-    def act_grads(g, a, b, sig, silu, w):
-        dh = dot(g, wd[w], 1, 1)
+    def act_grads(g, a, b, sig, silu, down):
+        dh = dot(g, wd[down], 1, 1)
         return (dh * b * sig * (1.0 + a * (1.0 - sig))).astype(BF16), (dh * silu).astype(BF16)
 
     def weight_grads(x, h, g, da, db, e):
@@ -165,16 +168,16 @@
         dwg[e] += dot(x, da, 0, 0)
         dwu[e] += dot(x, db, 0, 0)
 
-    def column_task(r, w, eid, first, grads):
+    def column_task(r, w, down, eid, first, grads):
         gate = gate_column([gtc[r, 0], gtc[r, 1]], eid)
         x = xyc[r, 0].reshape(tok, d_model)
         dy32 = xyc[r, 1].reshape(tok, d_model).astype(F32)
         a, b, sig, silu, h = acts(x, gate, w)
-        o = dot(h, wd[w], 1, 0).astype(BF16).astype(F32)
+        o = dot(h, wd[down], 1, 0).astype(BF16).astype(F32)
         yc = (gate * o).reshape(2, th, d_model)
         dg = jnp.sum(dy32 * o, axis=1, keepdims=True)
         g = (gate * dy32).astype(BF16)
-        da, db = act_grads(g, a, b, sig, silu, w)
+        da, db = act_grads(g, a, b, sig, silu, down)
         dxc = (dot(da, wg[w], 1, 1) + dot(db, wu[w], 1, 1)).astype(BF16).astype(F32).reshape(2, th, d_model)
 
         if first is not None:
@@ -226,7 +229,7 @@
             arrive(*two('x2'), 'x2g')
             start(*[(n, 1, d) for d in both for n in ('y3', 'y3g')])
 
-        column_task(r, e, expert_id(e, 0), e == 0, e)
+        column_task(r, e, e, expert_id(e, 0), e == 0, e)
 
     loop(2 * SIDE, own_step)
 
@@ -241,8 +244,8 @@
         for m in ms:
             weight_load(p, i, slot, m).start()
 
-    def load_wait(p, i, slot):
-        for m in mats:
+    def load_wait(p, i, slot, ms=mats):
+        for m in ms:
             weight_load(p, i, slot, m).wait()
 
     def early_step(t):
@@ -300,17 +303,18 @@
                 arrive(*[('w2', m, d) for m in both for d in both])
                 start(*two('m', 2))
                 load_start(0, 2, 2, both)
-
-        column_task(r, slot, expert_id(p, i), None, None)
+                pl.semaphore_signal(slot_sem, inc=1, device_id=mate, device_id_type=MESH)
+
+        column_task(r, slot, slot, expert_id(p, i), None, None)
 
     loop(13, near_step)
 
-    arrive(*two('w2', 2))
-    start(('m', 2, 2))
-    load_start(0, 2, 2, (2,))
     arrive(*two('m', 2))
     load_start(1, 2, 3, both)
-    load_wait(0, 2, 2)
+    load_wait(0, 2, 2, both)
+    arrive(*two('w2', 2))
+    pl.semaphore_wait(slot_sem, 1)
+    start(('m', 2, 2))
 
     def far_step(t):
         u, p = t // 2, t % 2
@@ -318,9 +322,8 @@
 
         @at_step(t, 1)
         def _():
+            load_wait(1, 2, 3, both)
             arrive(('m', 2, 2))
-            load_start(1, 2, 3, (2,))
-            load_wait(1, 2, 3)
 
         @at_step(t, 2)
         def _():
@@ -330,7 +333,7 @@
         def _():
             start(('r2', 1, 0), ('r2g', 1, 0), ('r2', 0, 1), ('r2g', 0, 1))
 
-        column_task(r, 2 + p, expert_id(p, 2), None, None)
+        column_task(r, 2 + p, FAR - 2 * p, expert_id(p, 2), None, None)
 
     loop(2 * SIDE, far_step)
 
@@ -356,7 +359,7 @@
     def last_step(v):
         p, i, slot = near_expert(v)
         load_wait(p, i, slot)
-        column_task(0, slot, expert_id(p, i), None, None)
+        column_task(0, slot, slot, expert_id(p, i), None, None)
 
         @at_step(v, 0)
         def _():
@@ -406,12 +409,20 @@
         ((dwg, dwg_out), (dwu, dwu_out), (dwd, dwd_out)))]
     for store in stores:
         store.start()
-    arrive(*[(n, h, d) for h in both for d in both for n in ('r2', 'r2g')])
+    msgs.pop(('m', 2, 2)).wait_send()
     for h in both:
+        d = 1 - h
+        arrive(('r2', h, d), ('r2g', h, d))
+        con[0, :, h] += rsf[d, :, h]
+        cong[0, h] += rsfg[d, h]
+    for h in both:
+        arrive(('r2', h, h), ('r2g', h, h))
         rows = pl.ds(h * th, th)
-        y_out[rows, :] = (con[0, 0, h] + rsf[0, 0, h] + rsf[1, 0, h]).astype(BF16)
-        dx_out[rows, :] = (con[0, 1, h] + rsf[0, 1, h] + rsf[1, 1, h]).astype(BF16)
-        dgt_out[h] = cong[0, h] + rsfg[0, h] + rsfg[1, h]
+        for k, out in enumerate((y_out, dx_out)):
+            wd[FAR, pl.ds(k * tok + h * th, th)] = (con[0, k, h] + rsf[h, k, h]).astype(BF16)
+            stores.append(pltpu.make_async_copy(wd.at[FAR, pl.ds(k * tok + h * th, th)], out.at[rows], loc_sem.at[4 + 2 * k + h]))
+            stores[-1].start()
+        dgt_out[h] = cong[0, h] + rsfg[h, h]
     arrive(*[('dw', m) for m in mats])
     for c in msgs.values():
         c.wait_send()
@@ -469,7 +480,7 @@
                 shape((2, d_model, d_ff), F32), shape((2, d_model, d_ff), F32), shape((2, d_ff, d_model), F32),
                 shape((2, SIDE, d_model, d_ff), BF16), shape((2, SIDE, d_model, d_ff), BF16), shape((2, SIDE, d_ff, d_model), BF16)),
             in_specs=[hbm] * 6,
-            out_specs=(vmem,) * 3 + (hbm,) * 6,
+            out_specs=(hbm,) * 2 + (vmem,) + (hbm,) * 6,
             scratch_shapes=[
                 pltpu.VMEM((SIDE, 2, 2, th, d_model), BF16),
                 pltpu.VMEM((SIDE - 1, 2, 2, SIDE, th, d_model), BF16),
@@ -481,9 +492,9 @@
                 pltpu.VMEM((2, pk, LANES), F32),
                 pltpu.VMEM((2, 2, 2, th, d_model), F32),
                 pltpu.VMEM((2, 2, pk, LANES), F32),
-                pltpu.VMEM((4, d_model, d_ff), BF16), pltpu.VMEM((4, d_model, d_ff), BF16), pltpu.VMEM((4, d_ff, d_model), BF16),
+                pltpu.VMEM((FAR, d_model, d_ff), BF16), pltpu.VMEM((FAR, d_model, d_ff), BF16), pltpu.VMEM((FAR + 1, d_ff, d_model), BF16),
                 pltpu.VMEM((2, d_model, d_ff), F32), pltpu.VMEM((2, d_model, d_ff), F32), pltpu.VMEM((2, d_ff, d_model), F32),
-                dma((N_MSG,)), dma((N_MSG,)), dma((6,)), dma((2, 3)), pltpu.SemaphoreType.REGULAR,
+                dma((N_MSG,)), dma((N_MSG,)), dma((8,)), dma((2, 3)), pltpu.SemaphoreType.REGULAR, pltpu.SemaphoreType.REGULAR,
             ],
             compiler_params=pltpu.CompilerParams(collective_id=0, has_side_effects=True, vmem_limit_bytes=67000000),
             cost_estimate=pl.CostEstimate(flops=2 * units * tok * d_model * d_ff, bytes_accessed=64 * tok * d_model, transcendentals=0),

time: 224 us -> 224 us (level)
  no operation moved by 1% of the time
where the time goes in v6:
time: 224 us
  Pallas kernels  220 us (98%)
    pallas_call x1, Pallas kernels, device_layer(): pl.pallas_call(kernel, out_shape=(shape((tok, d_model), BF16), shape((tok...  212 us
    pallas_call x1, Pallas kernels, device_layer(): pl.pallas_call(functools.partial(finish, cut), out_shape=(shape((1,) + wi...  7.81 us

profile of v6, /device:TPU:97, one launch (start us, length us, event | category | flops | bytes accessed | tf_op | source)
XLA Modules:
  0.0 223.6 jit_solution(6701054847789079080)
XLA Ops:
  0.6 0.8 select_reduce_fusion.1
  1.4 0.1 reshape.32
  1.5 0.1 copy.20
  1.6 0.7 reshape.33.gt_hbm
  2.4 212.4 %shard_map.118 = (bf16[256,1024]{1,0:T(8,128)(2,1)}, bf16[256,1024]{1,0:T(8,128)(2,1)}, f32[2,32,128]{2,1,0:T(8,128)}, f32[2,1024,512]{2,1,0:T(8,128)}, f32[2,10...) custom-call(bf16[2,128,1024]{2,1,0:T(8,128)(2,1)} %bitcast.16, ...), custom_call_target="tpu_custom_call" | custom-call | flops 154618822656 | bytes 16777216 | tf_op jit(solution)/shard_map/pallas_call | solution.py:476
  214.8 0.0 copy-start
  214.8 0.0 copy-start.1
  214.8 7.8 %shard_map.119 = (f32[1,1024,512]{2,1,0:T(8,128)}, f32[1,1024,512]{2,1,0:T(8,128)}, f32[1,512,1024]{2,1,0:T(8,128)}, bf16[256,1024]{1,0:T(8,128)(2,1)}, bf16[256,1024]{1,0:T(8,128)(2,1)}) custom-call(f32[2,1024,512]{2,1,0:T(8,128)} %get-tuple-element.17.dwg_in, f32[2,1024,512]{2,1,0:T(8,128)} %get-tuple-element.18.dwu_in, ...), custom_call_target="tpu_custom_call" | custom-call | flops 1572864 | bytes 18874368 | tf_op jit(solution)/shard_map/pallas_call | solution.py:505
  222.6 0.0 copy-done
  222.6 0.1 reshape.34
  222.7 0.1 copy.21
  222.9 0.1 broadcast_in_dim.29
  223.0 0.0 copy-done.1
  223.0 0.6 select_reduce_fusion
Async XLA Ops:
  214.8 7.8 %copy-start = (f32[2,32,128]{2,1,0:T(8,128)S(1)}, f32[2,32,128]{2,1,0:T(8,128)}, u32[]{:S(2)}) copy-start(f32[2,32,128]{2,1,0:T(8,128)} %get-tuple-element.24) | copy-start | bytes 98308
  214.8 8.2 %copy-start.1 = (s32[256,8]{0,1:T(8,128)S(1)}, s32[256,8]{0,1:T(8,128)}, u32[]{:S(2)}) copy-start(s32[256,8]{0,1:T(8,128)} %param.8) | copy-start | bytes 24580
